TPU v7x, 32 devices: a whole 2x2x4 slice. The times are simulated.
32 devices in a mesh: freq: 8 (over z, y), rows: 4 (over x, core).
Axes of the slice: x: 2, y: 2, z: 4, core: 2. Of those that a mesh axis runs over, the one named last changes fastest.
Arguments:
- wavefield: bfloat16 [10240, 32, 1024], P('freq', 'rows'), may hold values from -6 to 6
- u_factors: bfloat16 [2, 16, 4, 256, 512], P(None, 'freq', 'rows'), may hold values from -0.25 to 0.25
- v_factors: bfloat16 [2, 16, 4, 512, 256], P(None, 'freq', 'rows'), may hold values from -0.375 to 0.375
- tile_ranks: int32 [16, 4, 40], P('freq', 'rows'), may hold values from 1 to 64, as said below
- tile_offsets: int32 [16, 4, 40], P('freq', 'rows'), may hold values from 0 to 511, as said below
Outputs:
- convolved: bfloat16 [1024, 32, 1024], P(('rows', 'freq'))
Inputs may be any that keep to these rules, and one draw needn't show every extreme that they name: tile_ranks[k, i, j] is the rank of tile (i, j) of frequency k; the ranks of one tile row sum to at most 512, exactly 512 on some row of every draw, and every tile row has a tile of rank 64. tile_offsets[k, i, j] is the sum of tile_ranks[k, i, j2] over j2 < j.
All inputs are finite; a program needn't handle non-finite values.
Results may differ from a plain program's by a relative error of at most 0.0072.
Values may be sent and summed in bfloat16 or wider, within the bound.
No kernel may reach another device: no remote copies, remote signals or barrier semaphores. Data moves between devices by JAX's collectives and lax.ppermute only.
A program may use at most 128 MiB of HBM per device.

v0:
```python
import functools
import math

import jax
import jax.numpy as jnp
from jax import lax
from jax.experimental import pallas as pl
from jax.experimental.pallas import tpu as pltpu
from jax.sharding import PartitionSpec as P


RANK_MAX = 64
LANES = 128
SUBLANES = 8
NT = (((1,), (1,)), ((), ()))
VMEM = pl.BlockSpec(memory_space=pltpu.VMEM)
SMEM = pl.BlockSpec(memory_space=pltpu.SMEM)
LATE = 2
PAIRED = (4, 8, 16)
AHEAD = 3


def spectral_tables(freq_count, sample_count):
    freq_bins = jnp.arange(freq_count, dtype=jnp.int32) + 1
    sample_index = jnp.arange(sample_count, dtype=jnp.int32)
    phase_int = freq_bins[:, None] * sample_index[None, :] % sample_count
    angles = phase_int.astype(jnp.float32) * (2.0 * math.pi / sample_count)
    cosine = jnp.cos(angles)
    minus_sine = -jnp.sin(angles)
    stacked = jnp.stack([cosine, minus_sine], axis=1)
    forward = (stacked / math.sqrt(sample_count)).astype(jnp.bfloat16)
    inverse = (stacked / math.sqrt(freq_count)).astype(jnp.bfloat16)
    return (forward, inverse)


def tile_windows(v_row, u_row, starts, rank_max):
    columns = starts.shape[0]
    slot_index = (starts[:, None] + jnp.arange(rank_max, dtype=jnp.int32)[None, :]).reshape(-1)
    v_padded = jnp.pad(v_row, ((0, 0), (0, rank_max), (0, 0)))
    u_padded = jnp.pad(u_row, ((0, 0), (0, 0), (0, rank_max)))
    v_win = jnp.take(v_padded, slot_index, axis=1).reshape(2, columns, rank_max, v_row.shape[2])
    u_win = jnp.take(u_padded, slot_index, axis=2).reshape(2, u_row.shape[1], columns, rank_max)
    return (v_win, u_win)


def slot_lookup(starts, counts, rank_max, slot_count):
    position = jnp.arange(slot_count, dtype=jnp.int32)
    started = starts[:, None, :] <= position[None, :, None]
    owner_tile = jnp.sum(started.astype(jnp.int32), axis=2) - 1
    first_slot = jnp.max(jnp.where(started, starts[:, None, :], 0), axis=2)
    within = position[None, :] - first_slot
    live_slot = position[None, :] < (starts[:, -1] + counts[:, -1])[:, None]
    flat_index = jnp.where(live_slot, owner_tile * rank_max + within, 0)
    return (flat_index, live_slot)


def take_slots(values, chosen):
    return jnp.take(values, chosen, axis=1)


def per_device(wavefield, u_factors, v_factors, tile_ranks, tile_offsets):
    rec_dev, src_dev, samples = wavefield.shape
    freq_dev = u_factors.shape[1]
    rows_dev = u_factors.shape[2]
    tile_size = u_factors.shape[3]
    slot_count = u_factors.shape[4]
    freq_group = lax.axis_size("freq")
    row_group = lax.axis_size("rows")
    freqs = freq_dev * freq_group
    receivers = rec_dev * freq_group
    columns = receivers // tile_size
    sources = src_dev * row_group
    forward, inverse = spectral_tables(freqs, samples)
    spectrum = jnp.einsum("kct,rst->kcrs", forward, wavefield, preferred_element_type=jnp.float32)
    spectrum = spectrum.astype(jnp.bfloat16).reshape(freqs, 2, rec_dev * src_dev)
    windows = jax.vmap(
        functools.partial(tile_windows, rank_max=RANK_MAX), in_axes=(1, 1, 0), out_axes=(1, 1)
    )
    rank_slots = jnp.arange(RANK_MAX, dtype=jnp.int32)
    tile_row = 0
    v_win, u_win = windows(
        v_factors[:, :, tile_row], u_factors[:, :, tile_row], tile_offsets[:, tile_row]
    )
    rank_mask = rank_slots[None, None, :] < tile_ranks[:, tile_row, :, None]
    flat_index, live_slot = slot_lookup(
        tile_offsets[:, tile_row], tile_ranks[:, tile_row], RANK_MAX, slot_count
    )
    prepared = [(v_win, u_win, rank_mask, flat_index, live_slot)]
    by_frequency = lax.all_to_all(spectrum, "freq", split_axis=0, concat_axis=2, tiled=True)
    portion = lax.all_gather(by_frequency[None], "rows", axis=0, tiled=True)
    blocks_in = portion.shape[0]
    spectra = portion.reshape(blocks_in, freq_dev, 2, columns, tile_size, src_dev)
    spectra = jnp.transpose(spectra, (1, 2, 3, 4, 0, 5)).reshape(
        freq_dev, 2, columns, tile_size, blocks_in * src_dev
    )
    tile_row = 0
    v_win, u_win, rank_mask, flat_index, live_slot = prepared[tile_row]
    quadrants = jnp.einsum(
        "afjmr,fbjrs->fabjms", v_win, spectra, preferred_element_type=jnp.float32
    )
    coeffs = jnp.stack(
        [quadrants[:, 0, 0] - quadrants[:, 1, 1], quadrants[:, 0, 1] + quadrants[:, 1, 0]], axis=1
    )
    coeffs = jnp.where(rank_mask[:, None, :, :, None], coeffs, 0.0).astype(jnp.bfloat16)
    stacked = coeffs.reshape(freq_dev, 2, columns * RANK_MAX, blocks_in * src_dev)
    packed = jax.vmap(take_slots)(stacked, flat_index)
    packed = jnp.where(live_slot[:, None, :, None], packed, jnp.zeros((), jnp.bfloat16))
    products = jnp.einsum(
        "afrk,fcks->facrs", u_factors[:, :, tile_row], packed, preferred_element_type=jnp.float32
    )
    results = [
        jnp.stack(
            [products[:, 0, 0] - products[:, 1, 1], products[:, 0, 1] + products[:, 1, 0]], axis=1
        )
    ]
    merged = jnp.stack(results, axis=2)
    bands = merged.astype(jnp.bfloat16).reshape(
        freq_dev, 2, rows_dev * tile_size, blocks_in, src_dev
    )
    bands = bands.reshape(freq_dev, 2, rows_dev * tile_size * sources)
    returned = lax.all_to_all(bands, "freq", split_axis=2, concat_axis=0, tiled=True)
    series = jnp.einsum("kcq,kct->qt", returned, inverse, preferred_element_type=jnp.float32)
    return series.astype(jnp.bfloat16).reshape(rows_dev * tile_size // freq_group, sources, samples)


def transform_kernel(traces_ref, table_ref, *refs):
    groups = lax.axis_size("freq")
    outs, (traces, sems, products, turned) = refs[:groups], refs[groups:]
    me = lax.axis_index("freq")
    rows = products.shape[1]
    kinds = turned.shape[0] // SUBLANES
    packs = LANES // kinds
    blocks = traces_ref.shape[0] // rows
    each = outs[0].shape[0]

    def copy(i):
        part = pl.ds(pl.multiple_of(i * rows, rows), rows)
        return pltpu.make_async_copy(traces_ref.at[part, :], traces.at[part, :], sems.at[i])

    def turn(i, source_rows):
        place = lax.broadcasted_iota(jnp.int32, (rows // SUBLANES, LANES), 1) // kinds
        for first in range(0, SUBLANES, packs):
            mixed = source_rows[pl.ds(first, rows // SUBLANES, stride=SUBLANES), :]
            for m in range(1, packs):
                part = source_rows[pl.ds(first + m, rows // SUBLANES, stride=SUBLANES), :]
                mixed = jnp.where(place == m, part, mixed)
            mixed = mixed.T
            for m in range(packs):
                turned[pl.ds(first + m, kinds, stride=SUBLANES), :] = mixed[
                    m * kinds : (m + 1) * kinds
                ]
        lanes = pl.ds(pl.multiple_of(i * LANES, LANES), LANES)
        for shift, out in enumerate(outs):
            group = me ^ shift
            start = pl.multiple_of(group * each, each)
            out[:, lanes] = turned[pl.ds(start, each), :].astype(jnp.bfloat16)

    for i in range(min(AHEAD, blocks)):
        copy(i).start()

    def step(i, carry):
        now = lax.rem(i, 2)

        @pl.when(i + AHEAD < blocks)
        def _():
            copy(i + AHEAD).start()

        copy(i).wait()
        part = pl.ds(pl.multiple_of(i * rows, rows), rows)
        turn(jnp.maximum(i - 1, 0), products.at[1 - now])
        products[now] = lax.dot_general(
            traces[part, :], table_ref[...], NT, preferred_element_type=jnp.float32
        )
        return carry

    lax.fori_loop(0, blocks, step, 0)
    turn(blocks - 1, products.at[(blocks - 1) % 2])


def transform(traces, table, groups):
    rows, samples = traces.shape
    receivers = rows // SUBLANES
    kinds = table.shape[0]
    repeated = jnp.tile(table, (LANES // kinds, 1))
    shape = jax.ShapeDtypeStruct((kinds * SUBLANES // groups, receivers), jnp.bfloat16)
    return pl.pallas_call(
        transform_kernel,
        in_specs=[pl.BlockSpec(memory_space=pltpu.HBM), VMEM],
        out_specs=[VMEM] * groups,
        out_shape=[shape] * groups,
        scratch_shapes=[
            pltpu.VMEM((rows, samples), jnp.bfloat16),
            pltpu.SemaphoreType.DMA((receivers // LANES,)),
            pltpu.VMEM((2, LANES * SUBLANES, LANES), jnp.float32),
            pltpu.VMEM((kinds * SUBLANES, LANES), jnp.float32),
        ],
        compiler_params=pltpu.CompilerParams(vmem_limit_bytes=48 * 2**20),
        cost_estimate=pl.CostEstimate(
            flops=2 * rows * samples * 256, bytes_accessed=rows * samples * 2, transcendentals=0
        ),
        name="transform",
    )(traces, repeated)


def coefficient_kernel(shifts, sides, before, *refs):
    count = len(shifts)
    refs = list(refs)
    offsets = [refs.pop(0) for _ in range(sides)]
    own = [refs.pop(0) for _ in range(count)]
    twin = [refs.pop(0) for _ in range(count)]
    factors = [refs.pop(0) for _ in range(sides)]
    earlier = [refs.pop(0) for _ in range(before)]
    outs = [refs.pop(0) for _ in range(sides)]
    (lhs,) = refs
    groups = lax.axis_size("freq")
    me = lax.axis_index("freq")
    core = lax.rem(lax.axis_index("rows"), 2)
    _, freqs, slots, tile = factors[0].shape
    per_block = own[0].shape[1] // tile
    columns = groups * per_block
    half = 2 * SUBLANES
    deep = 2 * half
    for k in range(freqs):
        for arrays, at in ((own, core), (twin, 1 - core)):
            for b in range(count):
                for inner in range(per_block):
                    start = (b * per_block + inner) * deep + at * half
                    lhs[k, pl.ds(pl.multiple_of(start, half), half), :] = arrays[b][
                        k * half : (k + 1) * half, inner * tile : (inner + 1) * tile
                    ]
    for side in range(sides):
        for k in range(freqs):
            for low in range(0, slots, tile):
                slot = lax.broadcasted_iota(jnp.int32, (deep, tile), 1) + low
                chosen = []
                for part in range(2):
                    products = lax.dot_general(
                        lhs[k],
                        factors[side][part, k, low : low + tile, :],
                        NT,
                        preferred_element_type=jnp.float32,
                    )
                    total = jnp.zeros((deep, tile), jnp.float32)
                    for b, shift in enumerate(shifts):
                        column = (me ^ shift) * per_block
                        value = total
                        for inner in range(per_block):
                            at = (b * per_block + inner) * deep
                            value = jnp.where(
                                slot >= offsets[side][k, 0, column + inner],
                                products[at : at + deep],
                                value,
                            )
                        after = jnp.minimum(column + per_block, columns - 1)
                        end = jnp.where(
                            column + per_block < columns, offsets[side][k, 0, after], slots
                        )
                        total = jnp.where(slot >= end, total, value)
                    chosen.append(total)
                by_real, by_imag = chosen
                n = SUBLANES
                real = [by_real[g : g + n] - by_imag[g + n : g + 2 * n] for g in (0, half)]
                imag = [by_real[g + n : g + 2 * n] + by_imag[g : g + n] for g in (0, half)]
                for c, pieces in enumerate((real, imag)):
                    value = jnp.concatenate(pieces, 0)
                    if side < before:
                        value += earlier[side][k, c, :, low : low + tile].astype(jnp.float32)
                    outs[side][k, c, :, low : low + tile] = value.astype(jnp.bfloat16)


def coefficients(shifts, offsets, own, twin, factors, earlier=()):
    sides, count = len(offsets), len(shifts)
    _, freqs, slots, tile = factors[0].shape
    columns = count * own[0].shape[1] // tile
    shape = jax.ShapeDtypeStruct((freqs, 2, 2 * SUBLANES, slots), jnp.bfloat16)
    return pl.pallas_call(
        functools.partial(coefficient_kernel, tuple(shifts), sides, len(earlier)),
        in_specs=[SMEM] * sides + [VMEM] * (2 * count + sides + len(earlier)),
        out_specs=[VMEM] * sides,
        out_shape=[shape] * sides,
        scratch_shapes=[pltpu.VMEM((freqs, columns * 4 * SUBLANES, tile), jnp.bfloat16)],
        compiler_params=pltpu.CompilerParams(vmem_limit_bytes=16 * 2**20),
        cost_estimate=pl.CostEstimate(
            flops=2 * 2 * sides * freqs * slots * columns * 4 * SUBLANES * tile,
            bytes_accessed=2**20,
            transcendentals=0,
        ),
        name="coefficients",
    )(*offsets, *own, *twin, *factors, *earlier)


def band_kernel(add, at_near, offsets_ref, ranks_ref, coeffs_ref, u_ref, *refs):
    refs = list(refs)
    other_ref = refs.pop(0) if add else None
    out_ref, rhs, crossed = refs[:3]
    freqs, _, sources, slots = coeffs_ref.shape
    tile = u_ref.shape[2]
    place = lax.rem(lax.axis_index("rows") // 2, 2)
    at = place if at_near else 1 - place
    last = offsets_ref.shape[2] - 1
    wide = 2 * sources
    rhs[...] = jnp.zeros_like(rhs)
    crossed[...] = jnp.zeros_like(crossed)
    slot = lax.broadcasted_iota(jnp.int32, (sources, slots), 1)
    for k in range(freqs):
        live = slot < offsets_ref[k, 0, last] + ranks_ref[k, 0, last]
        for part in range(2):
            value = jnp.where(live, coeffs_ref[k, part].astype(jnp.float32), 0.0)
            start = pl.multiple_of((2 * k + part) * wide + at * sources, sources)
            rhs[k, pl.ds(start, sources), :] = value.astype(jnp.bfloat16)
            start = pl.multiple_of((2 * k + 1 - part) * wide + at * sources, sources)
            value = value if part == 0 else -value
            crossed[k, pl.ds(start, sources), :] = value.astype(jnp.bfloat16)
    total = other_ref[...] if add else jnp.zeros((tile, 2 * freqs * wide), jnp.float32)
    for k in range(freqs):
        for part, ref in enumerate((rhs, crossed)):
            total += lax.dot_general(u_ref[part, k], ref[k], NT, preferred_element_type=jnp.float32)
    if not add:
        out_ref[...] = total
        return
    bands, mix = refs[3:]
    groups = out_ref.shape[0]
    bands[...] = total
    packs = LANES // wide
    kinds = 2 * freqs
    block = lax.broadcasted_iota(jnp.int32, (tile // packs, LANES), 1) // wide
    loaded = [bands[pl.ds(b, tile // packs, stride=packs), :] for b in range(packs)]
    rows = tile // packs // groups
    for kind in range(kinds):
        mixed = jnp.zeros((tile // packs, LANES), jnp.float32)
        for b in range(packs):
            shift = (b - kind) * wide % LANES
            moved = pltpu.roll(loaded[b], shift, 1) if shift else loaded[b]
            mixed = jnp.where(block == b, moved, mixed)
        mix[:, kind * rows : (kind + 1) * rows, :] = mixed.reshape(groups, rows, LANES)
    out_ref[...] = mix[...].astype(jnp.bfloat16)


def bands_of(at_near, offsets, ranks, coeffs, u_own, groups, other=None):
    add = other is not None
    freqs, _, sources, slots = coeffs.shape
    tile = u_own.shape[2]
    rows = 2 * freqs * tile * 2 * sources // LANES // groups
    partial = jax.ShapeDtypeStruct((tile, LANES), jnp.float32)
    whole = jax.ShapeDtypeStruct((groups, rows, LANES), jnp.bfloat16)
    spread = pltpu.VMEM((freqs, LANES, slots), jnp.bfloat16)
    mixing = [pltpu.VMEM((tile, LANES), jnp.float32), pltpu.VMEM(whole.shape, jnp.float32)]
    return pl.pallas_call(
        functools.partial(band_kernel, add, at_near),
        in_specs=[SMEM] * 2 + [VMEM] * (3 if add else 2),
        out_specs=VMEM,
        out_shape=whole if add else partial,
        scratch_shapes=[spread, spread] + (mixing if add else []),
        compiler_params=pltpu.CompilerParams(vmem_limit_bytes=8 * 2**20),
        cost_estimate=pl.CostEstimate(
            flops=2 * 2 * freqs * tile * LANES * slots, bytes_accessed=2**20, transcendentals=0
        ),
        name="bands",
    )(offsets, ranks, coeffs, u_own, *([other] if add else []))


def series_kernel(scale, bands_ref, table_ref, out_ref, wide, done, sems):
    groups, rows, lanes = bands_ref.shape
    kinds = table_ref.shape[0]
    steps = groups * rows // kinds
    wide[...] = bands_ref[...].astype(jnp.float32).reshape(groups * rows, lanes) * scale
    copies = []
    for i in range(steps):
        part = wide[pl.ds(i, kinds, stride=steps), :]
        done[i] = jnp.dot(
            part.T.astype(jnp.bfloat16), table_ref[...], preferred_element_type=jnp.float32
        ).astype(jnp.bfloat16)
        copies.append(
            pltpu.make_async_copy(
                done.at[i], out_ref.at[i * lanes : (i + 1) * lanes, :], sems.at[i]
            )
        )
        copies[-1].start()
    for copy in copies:
        copy.wait()


def series_of(bands, table, scale):
    groups, rows, lanes = bands.shape
    kinds, samples = table.shape
    steps = groups * rows // kinds
    return pl.pallas_call(
        functools.partial(series_kernel, scale),
        in_specs=[VMEM] * 2,
        out_specs=pl.BlockSpec(memory_space=pl.ANY),
        out_shape=jax.ShapeDtypeStruct((steps * lanes, samples), jnp.bfloat16),
        scratch_shapes=[
            pltpu.VMEM((groups * rows, lanes), jnp.float32),
            pltpu.VMEM((steps, lanes, samples), jnp.bfloat16),
            pltpu.SemaphoreType.DMA((steps,)),
        ],
        compiler_params=pltpu.CompilerParams(vmem_limit_bytes=16 * 2**20),
        cost_estimate=pl.CostEstimate(
            flops=2 * steps * lanes * kinds * samples,
            bytes_accessed=steps * lanes * samples * 2,
            transcendentals=0,
        ),
        name="series",
    )(bands, table)


def fits(rec_dev, src_dev, samples, freq_dev, rows_dev, tile, slots, freq_group, row_group):
    kinds = 2 * freq_dev * freq_group
    ratio = math.sqrt(samples) / math.sqrt(freq_dev * freq_group)
    return (
        math.frexp(ratio)[0] == 0.5
        and math.sqrt(samples).is_integer()
        and src_dev == SUBLANES
        and row_group == 4
        and rows_dev == 1
        and freq_group in PAIRED
        and rec_dev % tile == 0
        and tile % (2 * LANES) == 0
        and slots % tile == 0
        and LANES % kinds == 0
        and SUBLANES % (LANES // kinds) == 0
        and 2 * freq_dev * src_dev * row_group == LANES
        and tile % (4 * SUBLANES * freq_group) == 0
    )


def shift_order(groups):
    return [(groups // 2 - 1 - 2 * i) % (groups - 1) + 1 for i in range(groups - 1)]


def arrivals(groups):
    order = shift_order(groups)
    late = [s for s in order if s >= groups // 2][-LATE:]
    return [0] + [s for s in order if s not in late], late


def per_device_fast(wavefield, u_factors, v_factors, tile_ranks, tile_offsets):
    rec_dev, src_dev, samples = wavefield.shape
    freq_dev = u_factors.shape[1]
    groups = lax.axis_size("freq")
    row_group = lax.axis_size("rows")
    freqs = freq_dev * groups
    sources = src_dev * row_group
    tile = u_factors.shape[3]
    across = [(i, i ^ 2) for i in range(row_group)]
    beside = [(i, i ^ 1) for i in range(row_group)]
    forward, _ = spectral_tables(freqs, samples)
    u_own, v_own = u_factors[:, :, 0], v_factors[:, :, 0]
    v_far = lax.ppermute(v_own, "rows", across)
    offsets_far = lax.ppermute(tile_offsets, "rows", across)
    table = forward.reshape(2 * freqs, samples)
    sent = transform(wavefield.reshape(rec_dev * src_dev, samples), table, groups)
    own = {0: sent[0]}
    for shift in shift_order(groups):
        swap = [(i, i ^ shift) for i in range(groups)]
        own[shift] = lax.ppermute(sent[shift], "freq", swap)
    early, late = arrivals(groups)
    own_early, own_late = [own[s] for s in early], [own[s] for s in late]
    twin_early = []
    for shift, block in zip(early, own_early):
        twin_early.append(lax.ppermute(block, "rows", beside))
    (near,) = coefficients(early, [tile_offsets], own_early, twin_early, [v_own])
    (leaving,) = coefficients(early, [offsets_far], own_early, twin_early, [v_far])
    own_late, near, leaving = lax.optimization_barrier((own_late, near, leaving))
    twin_late = [lax.ppermute(block, "rows", beside) for block in own_late]
    (leaving,) = coefficients(late, [offsets_far], own_late, twin_late, [v_far], [leaving])
    far = lax.ppermute(leaving, "rows", across)
    (near,) = coefficients(late, [tile_offsets], own_late, twin_late, [v_own], [near])
    half = bands_of(True, tile_offsets, tile_ranks, near, u_own, groups)
    bands = bands_of(False, tile_offsets, tile_ranks, far, u_own, groups, half)
    returned = lax.all_to_all(bands, "freq", split_axis=0, concat_axis=0, tiled=True)
    series = series_of(returned, table, math.sqrt(samples) / math.sqrt(freqs))
    return series.reshape(tile // groups, sources, samples)


def choose(wavefield, u_factors, v_factors, tile_ranks, tile_offsets):
    ok = fits(
        wavefield.shape[0],
        wavefield.shape[1],
        wavefield.shape[2],
        u_factors.shape[1],
        u_factors.shape[2],
        u_factors.shape[3],
        u_factors.shape[4],
        lax.axis_size("freq"),
        lax.axis_size("rows"),
    )
    step = per_device_fast if ok else per_device
    return step(wavefield, u_factors, v_factors, tile_ranks, tile_offsets)


def solution(mesh):
    placed = (
        P("freq", "rows", None),
        P(None, "freq", "rows", None, None),
        P(None, "freq", "rows", None, None),
        P("freq", "rows", None),
        P("freq", "rows", None),
    )
    return jax.shard_map(
        choose,
        mesh=mesh,
        in_specs=placed,
        out_specs=P(("rows", "freq"), None, None),
        check_vma=False,
    )
```

profile of v0, /device:TPU:0, one launch (start us, length us, event | category | flops | bytes accessed | tf_op | source)
XLA Modules:
  0.0 58.9 jit_solution(3451214376284578360)
XLA Ops:
  0.0 3.0 %collective-permute-start.14 = (bf16[2,2,512,256]{3,2,1,0:T(8,128)(2,1)}, bf16[2,2,512,256]{3,2,1,0:T(8,128)(2,1)S(1)}, u32[]{:S(2)}, u32[]{:S(2)}) collective-permute-start(bf16[2,2,512,256]{3,2,1,0:T(8,128)(2,1)} %bitcast.7), channel_id=1, source_target_pairs={{0,2},{1,3},{2,0},{3,1},{4,6},{5,7},{6,4},{7,5},{8,10},{9,11},{10,... | collective-permute-start | bytes 3145736 | tf_op jit(solution)/shard_map/ppermute | solution.py:449
  3.1 0.3 fusion.7
  3.6 9.6 %transform.1 = (bf16[32,1280]{1,0:T(8,128)(2,1)S(1)}, bf16[32,1280]{1,0:T(8,128)(2,1)S(1)}, bf16[32,1280]{1,0:T(8,128)(2,1)S(1)}, bf16[32,1280]{1,0:T(8,128)(2,1...) custom-call(bf16[10240,1024]{1,0:T(8,128)(2,1)} %bitcast.11, ...), custom_call_target="tpu_custom_call" | custom-call | flops 5368709120 | bytes 20971520 | tf_op jit(solution)/shard_map/transform/pallas_call | solution.py:186
  13.1 2.7 %collective-permute-start.3 = (bf16[32,1280]{1,0:T(8,128)(2,1)S(1)}, bf16[32,1280]{1,0:T(8,128)(2,1)S(1)}, u32[]{:S(2)}, u32[]{:S(2)}) collective-permute-start(bf16[32,1280]{1,0:T(8,128)(2,1)S(1)} %get-tuple-element.20), channel_id=1, source_target_pairs={{0,16},{4,20},{8,24},{12,28},{16,0},{20,4},{24,8},{28,12},{1,17},{... | collective-permute-start | bytes 245768 | tf_op jit(solution)/shard_map/ppermute | solution.py:456
  15.8 1.6 %collective-permute-start.4 = (bf16[32,1280]{1,0:T(8,128)(2,1)S(1)}, bf16[32,1280]{1,0:T(8,128)(2,1)S(1)}, u32[]{:S(2)}, u32[]{:S(2)}) collective-permute-start(bf16[32,1280]{1,0:T(8,128)(2,1)S(1)} %get-tuple-element.21), channel_id=1, source_target_pairs={{0,8},{4,12},{8,0},{12,4},{16,24},{20,28},{24,16},{28,20},{1,9},{5... | collective-permute-start | bytes 245768 | tf_op jit(solution)/shard_map/ppermute | solution.py:456
  17.4 1.2 %collective-permute-start.5 = (bf16[32,1280]{1,0:T(8,128)(2,1)S(1)}, bf16[32,1280]{1,0:T(8,128)(2,1)S(1)}, u32[]{:S(2)}, u32[]{:S(2)}) collective-permute-start(bf16[32,1280]{1,0:T(8,128)(2,1)S(1)} %get-tuple-element.22), channel_id=1, source_target_pairs={{0,28},{4,24},{8,20},{12,16},{16,12},{20,8},{24,4},{28,0},{1,29},{... | collective-permute-start | bytes 245768 | tf_op jit(solution)/shard_map/ppermute | solution.py:456
  18.5 0.6 %collective-permute-start.6 = (bf16[32,1280]{1,0:T(8,128)(2,1)S(1)}, bf16[32,1280]{1,0:T(8,128)(2,1)S(1)}, u32[]{:S(2)}, u32[]{:S(2)}) collective-permute-start(bf16[32,1280]{1,0:T(8,128)(2,1)S(1)} %get-tuple-element.23), channel_id=1, source_target_pairs={{0,12},{4,8},{8,4},{12,0},{16,28},{20,24},{24,20},{28,16},{1,13},{... | collective-permute-start | bytes 245768 | tf_op jit(solution)/shard_map/ppermute | solution.py:456
  19.2 0.1 collective-permute-done.3.refs_2_
  19.3 2.4 %collective-permute-start.7 = (bf16[32,1280]{1,0:T(8,128)(2,1)S(1)}, bf16[32,1280]{1,0:T(8,128)(2,1)S(1)}, u32[]{:S(2)}, u32[]{:S(2)}) collective-permute-start(bf16[32,1280]{1,0:T(8,128)(2,1)S(1)} %get-tuple-element.24), channel_id=1, source_target_pairs={{0,4},{4,0},{8,12},{12,8},{16,20},{20,16},{24,28},{28,24},{1,5},{5... | collective-permute-start | bytes 245768 | tf_op jit(solution)/shard_map/ppermute | solution.py:456
  21.7 3.0 %collective-permute-done.5.refs_4_ = bf16[32,1280]{1,0:T(8,128)(2,1)S(1)} collective-permute-done((bf16[32,1280]{1,0:T(8,128)(2,1)S(1)}, bf16[32,1280]{1,0:T(8,128)(2,1)S(1)}, u32[]{:S(2)}, u32[]{:S(2)}) %collective-permute-start.5) | collective-permute-done | bytes 81952 | tf_op jit(solution)/shard_map/ppermute | solution.py:456
  24.7 0.2 collective-permute-done.6.refs_5_
  25.0 0.3 collective-permute-start.10
  25.2 0.5 collective-permute-done.7.refs_6_
  25.7 0.5 collective-permute-start.12
  26.3 0.5 collective-permute-start
  26.8 0.2 collective-permute-done.11.refs_10_
  27.0 3.2 %collective-permute-start.1 = (bf16[32,1280]{1,0:T(8,128)(2,1)S(1)}, bf16[32,1280]{1,0:T(8,128)(2,1)S(1)}, u32[]{:S(2)}, u32[]{:S(2)}) collective-permute-start(bf16[32,1280]{1,0:T(8,128)(2,1)S(1)} %get-tuple-element.17), channel_id=1, source_target_pairs={{0,20},{4,16},{8,28},{12,24},{16,4},{20,0},{24,12},{28,8},{1,21},{... | collective-permute-start | bytes 245768 | tf_op jit(solution)/shard_map/ppermute | solution.py:456
  30.2 0.7 %collective-permute-start.2 = (bf16[32,1280]{1,0:T(8,128)(2,1)S(1)}, bf16[32,1280]{1,0:T(8,128)(2,1)S(1)}, u32[]{:S(2)}, u32[]{:S(2)}) collective-permute-start(bf16[32,1280]{1,0:T(8,128)(2,1)S(1)} %get-tuple-element.18), channel_id=1, source_target_pairs={{0,24},{4,28},{8,16},{12,20},{16,8},{20,12},{24,0},{28,4},{1,25},{... | collective-permute-start | bytes 245768 | tf_op jit(solution)/shard_map/ppermute | solution.py:456
  30.9 1.8 %coefficients.4.refs_6_ = bf16[2,2,16,512]{3,2,1,0:T(8,128)(2,1)S(1)} custom-call(s32[2,1,40]{2,1,0:T(1,128)S(1)} %copy-done.2, bf16[32,1280]{1,0:T(8,128)(2,1)S(1)} %get-tuple-element.19.refs_1_, bf16[32,1280]{1,0:T(8,128)(2,1)S(1)} %collective-permute-done.3.refs_2_, bf16[32,1280]{1,0:T(8,128)(2,1)S(1)} %collective-permute-done.4.refs_3_, ...), custom_call_target="tpu_custom_call" | custom-call | flops 1006632960 | bytes 1048576 | tf_op jit(solution)/shard_map/coefficients/pallas_call | solution.py:276
  32.7 1.8 %coefficients.5.refs_6_ = bf16[2,2,16,512]{3,2,1,0:T(8,128)(2,1)S(1)} custom-call(s32[2,1,40]{2,1,0:T(1,128)S(1)} %collective-permute-done.refs_0_, bf16[32,1280]{1,0:T(8,128)(2,1)S(1)} %get-tuple-element.19.refs_1_, bf16[32,1280]{1,0:T(8,128)(2,1)S(1)} %collective-permute-done.3.refs_2_, bf16[32,1280]{1,0:T(8,128)(2,1)S(1)} %collective-permute-done.4.refs_3_, ...), custom_call_target="tpu_custom_call" | custom-call | flops 1006632960 | bytes 1048576 | tf_op jit(solution)/shard_map/coefficients/pallas_call | solution.py:276
  34.5 3.1 %collective-permute-done.1.refs_1_ = bf16[32,1280]{1,0:T(8,128)(2,1)S(1)} collective-permute-done((bf16[32,1280]{1,0:T(8,128)(2,1)S(1)}, bf16[32,1280]{1,0:T(8,128)(2,1)S(1)}, u32[]{:S(2)}, u32[]{:S(2)}) %collective-permute-start.1) | collective-permute-done | bytes 81952 | tf_op jit(solution)/shard_map/ppermute | solution.py:456
  37.6 0.5 collective-permute-start.16
  38.1 0.8 %collective-permute-done.15.refs_3_ = bf16[32,1280]{1,0:T(8,128)(2,1)S(1)} collective-permute-done((bf16[32,1280]{1,0:T(8,128)(2,1)S(1)}, bf16[32,1280]{1,0:T(8,128)(2,1)S(1)}, u32[]{:S(2)}, u32[]{:S(2)}) %collective-permute-start.15) | collective-permute-done | bytes 81952 | tf_op jit(solution)/shard_map/ppermute | solution.py:465
  38.9 0.2 collective-permute-done.16.refs_4_
  39.0 1.1 %coefficients.6 = bf16[2,2,16,512]{3,2,1,0:T(8,128)(2,1)S(1)} custom-call(s32[2,1,40]{2,1,0:T(1,128)S(1)} %collective-permute-done.refs_0_, bf16[32,1280]{1,0:T(8,128)(2,1)S(1)} %collective-permute-done.1.refs_1_, bf16[32,1280]{1,0:T(8,128)(2,1)S(1)} %collective-permute-done.2.refs_2_, bf16[32,1280]{1,0:T(8,128)(2,1)S(1)} %collective-permute-done.15.refs_3_, ...), custom_call_target="tpu_custom_call" | custom-call | flops 335544320 | bytes 1048576 | tf_op jit(solution)/shard_map/coefficients/pallas_call | solution.py:276
  40.1 1.4 %collective-permute-start.17 = (bf16[2,2,16,512]{3,2,1,0:T(8,128)(2,1)S(1)}, bf16[2,2,16,512]{3,2,1,0:T(8,128)(2,1)S(1)}, u32[]{:S(2)}, u32[]{:S(2)}) collective-permute-start(bf16[2,2,16,512]{3,2,1,0:T(8,128)(2,1)S(1)} %coefficients.6), channel_id=1, source_target_pairs={{0,2},{1,3},{2,0},{3,1},{4,6},{5,7},{6,4},{7,5},{8,10},{9,11},{10,... | collective-permute-start | bytes 196616 | tf_op jit(solution)/shard_map/ppermute | solution.py:467
  41.6 1.1 %coefficients.7.coeffs_ref = bf16[2,2,16,512]{3,2,1,0:T(8,128)(2,1)S(1)} custom-call(s32[2,1,40]{2,1,0:T(1,128)S(1)} %copy-done.2, bf16[32,1280]{1,0:T(8,128)(2,1)S(1)} %collective-permute-done.1.refs_1_, bf16[32,1280]{1,0:T(8,128)(2,1)S(1)} %collective-permute-done.2.refs_2_, bf16[32,1280]{1,0:T(8,128)(2,1)S(1)} %collective-permute-done.15.refs_3_, ...), custom_call_target="tpu_custom_call" | custom-call | flops 335544320 | bytes 1048576 | tf_op jit(solution)/shard_map/coefficients/pallas_call | solution.py:276
  42.7 1.0 %bands.2.refs_0_ = f32[256,128]{1,0:T(8,128)S(1)} custom-call(s32[2,1,40]{2,1,0:T(1,128)S(1)} %copy-done.2, s32[2,1,40]{2,1,0:T(1,128)S(1)} %copy-done.3, bf16[2,2,16,512]{3,2,1,0:T(8,128)(2,1)S(1)} %coefficients.7.coeffs_ref, bf16[2,2,256,512]{3,2,1,0:T(8,128)(2,1)S(1)} %bitcast.5), custom_call_target="tpu_custom_call" | custom-call | flops 134217728 | bytes 1048576 | tf_op jit(solution)/shard_map/bands/pallas_call | solution.py:348
  43.7 0.9 %collective-permute-done.17.coeffs_ref = bf16[2,2,16,512]{3,2,1,0:T(8,128)(2,1)S(1)} collective-permute-done((bf16[2,2,16,512]{3,2,1,0:T(8,128)(2,1)S(1)}, bf16[2,2,16,512]{3,2,1,0:T(8,128)(2,1)S(1)}, u32[]{:S(2)}, u32[]{:S(2)}) %collective-permute-start.17) | collective-permute-done | bytes 65568 | tf_op jit(solution)/shard_map/ppermute | solution.py:467
  44.6 1.1 %bands.3 = bf16[8,32,128]{2,1,0:T(8,128)(2,1)S(1)} custom-call(s32[2,1,40]{2,1,0:T(1,128)S(1)} %copy-done.2, s32[2,1,40]{2,1,0:T(1,128)S(1)} %copy-done.3, bf16[2,2,16,512]{3,2,1,0:T(8,128)(2,1)S(1)} %collective-permute-done.17.coeffs_ref, bf16[2,2,256,512]{3,2,1,0:T(8,128)(2,1)S(1)} %bitcast.6, f32[256,128]{1,0:T(8,128)S(1)} %bands.2.refs_0_), custom_call_target="tpu_custom_call" | custom-call | flops 134217728 | bytes 1048576 | tf_op jit(solution)/shard_map/bands/pallas_call | solution.py:348
  45.7 11.5 %all_to_all.5.bands_ref = bf16[8,32,128]{2,1,0:T(8,128)(2,1)S(1)} all-to-all(bf16[8,32,128]{2,1,0:T(8,128)(2,1)S(1)} %bands.3), channel_id=1, replica_groups=mesh['freq'=8,'rows'=4] {'freq'}, dimensions={0} | all-to-all | bytes 131072 | tf_op jit(solution)/shard_map/all_to_all | solution.py:471
  57.2 1.7 %series.1 = bf16[1024,1024]{1,0:T(8,128)(2,1)} custom-call(bf16[8,32,128]{2,1,0:T(8,128)(2,1)S(1)} %all_to_all.5.bands_ref, bf16[32,1024]{1,0:T(8,128)(2,1)S(1)} %convert_element_type.29.table_ref), custom_call_target="tpu_custom_call" | custom-call | flops 67108864 | bytes 2097152 | tf_op jit(solution)/shard_map/series/pallas_call | solution.py:387
  (27 shorter events, 0.3 us)
Async XLA Ops:
  0.0 30.9 %copy-start.1 = (bf16[2,2,1,512,256]{4,3,2,1,0:T(8,128)(2,1)S(1)}, bf16[2,2,1,512,256]{4,3,2,1,0:T(8,128)(2,1)}, u32[]{:S(2)}) copy-start(bf16[2,2,1,512,256]{4,3,2,1,0:T(8,128)(2,1)} %param.7) | copy-start | bytes 3145732
  0.0 26.3 %copy-start.2 = (s32[2,1,40]{2,1,0:T(1,128)S(1)}, s32[2,1,40]{2,1,0:T(1,128)}, u32[]{:S(2)}) copy-start(s32[2,1,40]{2,1,0:T(1,128)} %offsets_ref.3) | copy-start | bytes 964
  0.0 42.7 %copy-start.3 = (s32[2,1,40]{2,1,0:T(1,128)S(1)}, s32[2,1,40]{2,1,0:T(1,128)}, u32[]{:S(2)}) copy-start(s32[2,1,40]{2,1,0:T(1,128)} %ranks_ref.3) | copy-start | bytes 964
  0.0 42.7 %copy-start = (bf16[2,2,1,256,512]{4,3,2,1,0:T(8,128)(2,1)S(1)}, bf16[2,2,1,256,512]{4,3,2,1,0:T(8,128)(2,1)}, u32[]{:S(2)}) copy-start(bf16[2,2,1,256,512]{4,3,2,1,0:T(8,128)(2,1)} %param.6) | copy-start | bytes 3145732
  0.0 32.7 %collective-permute-start.14 = (bf16[2,2,512,256]{3,2,1,0:T(8,128)(2,1)}, bf16[2,2,512,256]{3,2,1,0:T(8,128)(2,1)S(1)}, u32[]{:S(2)}, u32[]{:S(2)}) collective-permute-start(bf16[2,2,512,256]{3,2,1,0:T(8,128)(2,1)} %bitcast.7), channel_id=1, source_target_pairs={{0,2},{1,3},{2,0},{3,1},{4,6},{5,7},{6,4},{7,5},{8,10},{9,11},{10,... | collective-permute-start | bytes 3145736 | tf_op jit(solution)/shard_map/ppermute | solution.py:449
  13.1 6.2 %collective-permute-start.3 = (bf16[32,1280]{1,0:T(8,128)(2,1)S(1)}, bf16[32,1280]{1,0:T(8,128)(2,1)S(1)}, u32[]{:S(2)}, u32[]{:S(2)}) collective-permute-start(bf16[32,1280]{1,0:T(8,128)(2,1)S(1)} %get-tuple-element.20), channel_id=1, source_target_pairs={{0,16},{4,20},{8,24},{12,28},{16,0},{20,4},{24,8},{28,12},{1,17},{... | collective-permute-start | bytes 245768 | tf_op jit(solution)/shard_map/ppermute | solution.py:456
  15.8 5.9 %collective-permute-start.4 = (bf16[32,1280]{1,0:T(8,128)(2,1)S(1)}, bf16[32,1280]{1,0:T(8,128)(2,1)S(1)}, u32[]{:S(2)}, u32[]{:S(2)}) collective-permute-start(bf16[32,1280]{1,0:T(8,128)(2,1)S(1)} %get-tuple-element.21), channel_id=1, source_target_pairs={{0,8},{4,12},{8,0},{12,4},{16,24},{20,28},{24,16},{28,20},{1,9},{5... | collective-permute-start | bytes 245768 | tf_op jit(solution)/shard_map/ppermute | solution.py:456
  17.4 7.3 %collective-permute-start.5 = (bf16[32,1280]{1,0:T(8,128)(2,1)S(1)}, bf16[32,1280]{1,0:T(8,128)(2,1)S(1)}, u32[]{:S(2)}, u32[]{:S(2)}) collective-permute-start(bf16[32,1280]{1,0:T(8,128)(2,1)S(1)} %get-tuple-element.22), channel_id=1, source_target_pairs={{0,28},{4,24},{8,20},{12,16},{16,12},{20,8},{24,4},{28,0},{1,29},{... | collective-permute-start | bytes 245768 | tf_op jit(solution)/shard_map/ppermute | solution.py:456
  18.5 6.4 %collective-permute-start.6 = (bf16[32,1280]{1,0:T(8,128)(2,1)S(1)}, bf16[32,1280]{1,0:T(8,128)(2,1)S(1)}, u32[]{:S(2)}, u32[]{:S(2)}) collective-permute-start(bf16[32,1280]{1,0:T(8,128)(2,1)S(1)} %get-tuple-element.23), channel_id=1, source_target_pairs={{0,12},{4,8},{8,4},{12,0},{16,28},{20,24},{24,20},{28,16},{1,13},{... | collective-permute-start | bytes 245768 | tf_op jit(solution)/shard_map/ppermute | solution.py:456
  19.3 6.4 %collective-permute-start.7 = (bf16[32,1280]{1,0:T(8,128)(2,1)S(1)}, bf16[32,1280]{1,0:T(8,128)(2,1)S(1)}, u32[]{:S(2)}, u32[]{:S(2)}) collective-permute-start(bf16[32,1280]{1,0:T(8,128)(2,1)S(1)} %get-tuple-element.24), channel_id=1, source_target_pairs={{0,4},{4,0},{8,12},{12,8},{16,20},{20,16},{24,28},{28,24},{1,5},{5... | collective-permute-start | bytes 245768 | tf_op jit(solution)/shard_map/ppermute | solution.py:456
  21.7 4.0 %collective-permute-start.8 = (bf16[32,1280]{1,0:T(8,128)(2,1)S(1)}, bf16[32,1280]{1,0:T(8,128)(2,1)S(1)}, u32[]{:S(2)}, u32[]{:S(2)}) collective-permute-start(bf16[32,1280]{1,0:T(8,128)(2,1)S(1)} %get-tuple-element.19.refs_1_), channel_id=1, source_target_pairs={{0,1},{1,0},{2,3},{3,2},{4,5},{5,4},{6,7},{7,6},{8,9},{9,8},{10,11... | collective-permute-start | bytes 245768 | tf_op jit(solution)/shard_map/ppermute | solution.py:461
  24.7 1.5 %collective-permute-start.9 = (bf16[32,1280]{1,0:T(8,128)(2,1)S(1)}, bf16[32,1280]{1,0:T(8,128)(2,1)S(1)}, u32[]{:S(2)}, u32[]{:S(2)}) collective-permute-start(bf16[32,1280]{1,0:T(8,128)(2,1)S(1)} %collective-permute-done.3.refs_2_), channel_id=1, source_target_pairs={{0,1},{1,0},{2,3},{3,2},{4,5},{5,4},{6,7},{7,6},{8,9},{9,8},{10,11... | collective-permute-start | bytes 245768 | tf_op jit(solution)/shard_map/ppermute | solution.py:461
  25.0 1.4 %collective-permute-start.10 = (bf16[32,1280]{1,0:T(8,128)(2,1)S(1)}, bf16[32,1280]{1,0:T(8,128)(2,1)S(1)}, u32[]{:S(2)}, u32[]{:S(2)}) collective-permute-start(bf16[32,1280]{1,0:T(8,128)(2,1)S(1)} %collective-permute-done.4.refs_3_), channel_id=1, source_target_pairs={{0,1},{1,0},{2,3},{3,2},{4,5},{5,4},{6,7},{7,6},{8,9},{9,8},{10,11... | collective-permute-start | bytes 245768 | tf_op jit(solution)/shard_map/ppermute | solution.py:461
  25.7 1.3 %collective-permute-start.11 = (bf16[32,1280]{1,0:T(8,128)(2,1)S(1)}, bf16[32,1280]{1,0:T(8,128)(2,1)S(1)}, u32[]{:S(2)}, u32[]{:S(2)}) collective-permute-start(bf16[32,1280]{1,0:T(8,128)(2,1)S(1)} %collective-permute-done.5.refs_4_), channel_id=1, source_target_pairs={{0,1},{1,0},{2,3},{3,2},{4,5},{5,4},{6,7},{7,6},{8,9},{9,8},{10,11... | collective-permute-start | bytes 245768 | tf_op jit(solution)/shard_map/ppermute | solution.py:461
  25.7 4.5 %collective-permute-start.12 = (bf16[32,1280]{1,0:T(8,128)(2,1)S(1)}, bf16[32,1280]{1,0:T(8,128)(2,1)S(1)}, u32[]{:S(2)}, u32[]{:S(2)}) collective-permute-start(bf16[32,1280]{1,0:T(8,128)(2,1)S(1)} %collective-permute-done.6.refs_5_), channel_id=1, source_target_pairs={{0,1},{1,0},{2,3},{3,2},{4,5},{5,4},{6,7},{7,6},{8,9},{9,8},{10,11... | collective-permute-start | bytes 245768 | tf_op jit(solution)/shard_map/ppermute | solution.py:461
  26.3 4.6 %collective-permute-start.13 = (bf16[32,1280]{1,0:T(8,128)(2,1)S(1)}, bf16[32,1280]{1,0:T(8,128)(2,1)S(1)}, u32[]{:S(2)}, u32[]{:S(2)}) collective-permute-start(bf16[32,1280]{1,0:T(8,128)(2,1)S(1)} %collective-permute-done.7.refs_6_), channel_id=1, source_target_pairs={{0,1},{1,0},{2,3},{3,2},{4,5},{5,4},{6,7},{7,6},{8,9},{9,8},{10,11... | collective-permute-start | bytes 245768 | tf_op jit(solution)/shard_map/ppermute | solution.py:461
  26.3 6.3 %collective-permute-start = (s32[2,1,40]{2,1,0:T(1,128)S(1)}, s32[2,1,40]{2,1,0:T(1,128)S(1)}, u32[]{:S(2)}, u32[]{:S(2)}) collective-permute-start(s32[2,1,40]{2,1,0:T(1,128)S(1)} %copy-done.2), channel_id=1, source_target_pairs={{0,2},{1,3},{2,0},{3,1},{4,6},{5,7},{6,4},{7,5},{8,10},{9,11},{10,... | collective-permute-start | bytes 968 | tf_op jit(solution)/shard_map/ppermute | solution.py:450
  27.0 10.6 %collective-permute-start.1 = (bf16[32,1280]{1,0:T(8,128)(2,1)S(1)}, bf16[32,1280]{1,0:T(8,128)(2,1)S(1)}, u32[]{:S(2)}, u32[]{:S(2)}) collective-permute-start(bf16[32,1280]{1,0:T(8,128)(2,1)S(1)} %get-tuple-element.17), channel_id=1, source_target_pairs={{0,20},{4,16},{8,28},{12,24},{16,4},{20,0},{24,12},{28,8},{1,21},{... | collective-permute-start | bytes 245768 | tf_op jit(solution)/shard_map/ppermute | solution.py:456
  30.2 7.4 %collective-permute-start.2 = (bf16[32,1280]{1,0:T(8,128)(2,1)S(1)}, bf16[32,1280]{1,0:T(8,128)(2,1)S(1)}, u32[]{:S(2)}, u32[]{:S(2)}) collective-permute-start(bf16[32,1280]{1,0:T(8,128)(2,1)S(1)} %get-tuple-element.18), channel_id=1, source_target_pairs={{0,24},{4,28},{8,16},{12,20},{16,8},{20,12},{24,0},{28,4},{1,25},{... | collective-permute-start | bytes 245768 | tf_op jit(solution)/shard_map/ppermute | solution.py:456
  37.6 1.3 %collective-permute-start.15 = (bf16[32,1280]{1,0:T(8,128)(2,1)S(1)}, bf16[32,1280]{1,0:T(8,128)(2,1)S(1)}, u32[]{:S(2)}, u32[]{:S(2)}) collective-permute-start(bf16[32,1280]{1,0:T(8,128)(2,1)S(1)} %collective-permute-done.1.refs_1_), channel_id=1, source_target_pairs={{0,1},{1,0},{2,3},{3,2},{4,5},{5,4},{6,7},{7,6},{8,9},{9,8},{10,11... | collective-permute-start | bytes 245768 | tf_op jit(solution)/shard_map/ppermute | solution.py:465
  37.6 1.4 %collective-permute-start.16 = (bf16[32,1280]{1,0:T(8,128)(2,1)S(1)}, bf16[32,1280]{1,0:T(8,128)(2,1)S(1)}, u32[]{:S(2)}, u32[]{:S(2)}) collective-permute-start(bf16[32,1280]{1,0:T(8,128)(2,1)S(1)} %collective-permute-done.2.refs_2_), channel_id=1, source_target_pairs={{0,1},{1,0},{2,3},{3,2},{4,5},{5,4},{6,7},{7,6},{8,9},{9,8},{10,11... | collective-permute-start | bytes 245768 | tf_op jit(solution)/shard_map/ppermute | solution.py:465
  40.1 4.4 %collective-permute-start.17 = (bf16[2,2,16,512]{3,2,1,0:T(8,128)(2,1)S(1)}, bf16[2,2,16,512]{3,2,1,0:T(8,128)(2,1)S(1)}, u32[]{:S(2)}, u32[]{:S(2)}) collective-permute-start(bf16[2,2,16,512]{3,2,1,0:T(8,128)(2,1)S(1)} %coefficients.6), channel_id=1, source_target_pairs={{0,2},{1,3},{2,0},{3,1},{4,6},{5,7},{6,4},{7,5},{8,10},{9,11},{10,... | collective-permute-start | bytes 196616 | tf_op jit(solution)/shard_map/ppermute | solution.py:467
where the time goes:
time: 59 us; the launch traced here: 58.9 us
  Pallas kernels  19.1 us (32%)
  starting transfers between devices  18.6 us (32%)
  blocking collectives  11.5 us (19%)
  waiting for transfers between devices  8.98 us (15%)
    ppermute x7, starting transfers between devices, per_device_fast(): own[shift] = lax.ppermute(sent[shift], 'freq', swap)  12.3 us
    all_to_all x1, blocking collectives, per_device_fast(): lax.all_to_all(bands, 'freq', split_axis=0, concat_axis=0, tiled=True)  11.5 us
    pallas_call x1, Pallas kernels, transform(): pl.pallas_call(transform_kernel, in_specs=[pl.BlockSpec(memory_space=pltp...  9.56 us
    ppermute x7, waiting for transfers between devices, per_device_fast(): own[shift] = lax.ppermute(sent[shift], 'freq', swap)  7.01 us
    pallas_call x4, Pallas kernels, coefficients(): pl.pallas_call(functools.partial(coefficient_kernel, tuple(shifts), sides...  5.73 us
    ppermute x1, starting transfers between devices, per_device_fast(): v_far = lax.ppermute(v_own, 'rows', across)  3.04 us
    pallas_call x2, Pallas kernels, bands_of(): pl.pallas_call(functools.partial(band_kernel, add, at_near), in_specs=[SM...  2.13 us
    pallas_call x1, Pallas kernels, series_of(): pl.pallas_call(functools.partial(series_kernel, scale), in_specs=[VMEM] *...  1.65 us
  transfers between devices with their start and end apart: 18, of which 9 were waited for; matrix products, arithmetic and copies ran while one was open for 1% of the time, Pallas kernels for 26%

commit v1 on v0

--- a/solution.py
+++ b/solution.py
@@ -194,7 +194,7 @@
             pltpu.VMEM((2, LANES * SUBLANES, LANES), jnp.float32),
             pltpu.VMEM((kinds * SUBLANES, LANES), jnp.float32),
         ],
-        compiler_params=pltpu.CompilerParams(vmem_limit_bytes=48 * 2**20),
+        compiler_params=pltpu.CompilerParams(vmem_limit_bytes=45 * 2**20),
         cost_estimate=pl.CostEstimate(
             flops=2 * rows * samples * 256, bytes_accessed=rows * samples * 2, transcendentals=0
         ),
@@ -206,28 +206,25 @@
     count = len(shifts)
     refs = list(refs)
     offsets = [refs.pop(0) for _ in range(sides)]
-    own = [refs.pop(0) for _ in range(count)]
-    twin = [refs.pop(0) for _ in range(count)]
+    arrays = [refs.pop(0) for _ in range(count)]
     factors = [refs.pop(0) for _ in range(sides)]
     earlier = [refs.pop(0) for _ in range(before)]
     outs = [refs.pop(0) for _ in range(sides)]
     (lhs,) = refs
     groups = lax.axis_size("freq")
     me = lax.axis_index("freq")
-    core = lax.rem(lax.axis_index("rows"), 2)
     _, freqs, slots, tile = factors[0].shape
-    per_block = own[0].shape[1] // tile
+    per_block = arrays[0].shape[1] // tile
     columns = groups * per_block
-    half = 2 * SUBLANES
-    deep = 2 * half
+    n = SUBLANES
+    deep = 2 * n
     for k in range(freqs):
-        for arrays, at in ((own, core), (twin, 1 - core)):
-            for b in range(count):
-                for inner in range(per_block):
-                    start = (b * per_block + inner) * deep + at * half
-                    lhs[k, pl.ds(pl.multiple_of(start, half), half), :] = arrays[b][
-                        k * half : (k + 1) * half, inner * tile : (inner + 1) * tile
-                    ]
+        for b in range(count):
+            for inner in range(per_block):
+                start = (b * per_block + inner) * deep
+                lhs[k, start : start + deep, :] = arrays[b][
+                    k * deep : (k + 1) * deep, inner * tile : (inner + 1) * tile
+                ]
     for side in range(sides):
         for k in range(freqs):
             for low in range(0, slots, tile):
@@ -258,44 +255,44 @@
                         total = jnp.where(slot >= end, total, value)
                     chosen.append(total)
                 by_real, by_imag = chosen
-                n = SUBLANES
-                real = [by_real[g : g + n] - by_imag[g + n : g + 2 * n] for g in (0, half)]
-                imag = [by_real[g + n : g + 2 * n] + by_imag[g : g + n] for g in (0, half)]
-                for c, pieces in enumerate((real, imag)):
-                    value = jnp.concatenate(pieces, 0)
-                    if side < before:
-                        value += earlier[side][k, c, :, low : low + tile].astype(jnp.float32)
-                    outs[side][k, c, :, low : low + tile] = value.astype(jnp.bfloat16)
-
-
-def coefficients(shifts, offsets, own, twin, factors, earlier=()):
+                value = jnp.concatenate(
+                    [by_real[:n] - by_imag[n:], by_real[n:] + by_imag[:n]], axis=0
+                )
+                if side < before:
+                    value += earlier[side][k, :, low : low + tile].astype(jnp.float32)
+                outs[side][k, :, low : low + tile] = value.astype(jnp.bfloat16)
+
+
+def coefficients(shifts, offsets, arrays, factors, earlier=()):
     sides, count = len(offsets), len(shifts)
     _, freqs, slots, tile = factors[0].shape
-    columns = count * own[0].shape[1] // tile
-    shape = jax.ShapeDtypeStruct((freqs, 2, 2 * SUBLANES, slots), jnp.bfloat16)
+    rows = count * arrays[0].shape[1] // tile * 2 * SUBLANES
+    shape = jax.ShapeDtypeStruct((freqs, 2 * SUBLANES, slots), jnp.bfloat16)
     return pl.pallas_call(
         functools.partial(coefficient_kernel, tuple(shifts), sides, len(earlier)),
-        in_specs=[SMEM] * sides + [VMEM] * (2 * count + sides + len(earlier)),
+        in_specs=[SMEM] * sides + [VMEM] * (count + sides + len(earlier)),
         out_specs=[VMEM] * sides,
         out_shape=[shape] * sides,
-        scratch_shapes=[pltpu.VMEM((freqs, columns * 4 * SUBLANES, tile), jnp.bfloat16)],
-        compiler_params=pltpu.CompilerParams(vmem_limit_bytes=16 * 2**20),
+        scratch_shapes=[pltpu.VMEM((freqs, rows, tile), jnp.bfloat16)],
+        compiler_params=pltpu.CompilerParams(vmem_limit_bytes=12 * 2**20),
         cost_estimate=pl.CostEstimate(
-            flops=2 * 2 * sides * freqs * slots * columns * 4 * SUBLANES * tile,
+            flops=2 * 4 * sides * freqs * slots * rows * tile,
             bytes_accessed=2**20,
             transcendentals=0,
         ),
         name="coefficients",
-    )(*offsets, *own, *twin, *factors, *earlier)
-
-
-def band_kernel(add, at_near, offsets_ref, ranks_ref, coeffs_ref, u_ref, *refs):
+    )(*offsets, *arrays, *factors, *earlier)
+
+
+def band_kernel(add, at_near, offsets_ref, ranks_ref, same_ref, cross_ref, u_ref, *refs):
     refs = list(refs)
     other_ref = refs.pop(0) if add else None
     out_ref, rhs, crossed = refs[:3]
-    freqs, _, sources, slots = coeffs_ref.shape
+    freqs, sources, slots = same_ref.shape
     tile = u_ref.shape[2]
+    first = lax.rem(lax.axis_index("rows"), 2) == 0
     place = lax.rem(lax.axis_index("rows") // 2, 2)
+    n = SUBLANES
     at = place if at_near else 1 - place
     last = offsets_ref.shape[2] - 1
     wide = 2 * sources
@@ -304,8 +301,11 @@
     slot = lax.broadcasted_iota(jnp.int32, (sources, slots), 1)
     for k in range(freqs):
         live = slot < offsets_ref[k, 0, last] + ranks_ref[k, 0, last]
+        same, cross = same_ref[k].astype(jnp.float32), cross_ref[k].astype(jnp.float32)
+        low, high = jnp.where(first, same, cross), jnp.where(first, cross, same)
         for part in range(2):
-            value = jnp.where(live, coeffs_ref[k, part].astype(jnp.float32), 0.0)
+            rows = slice(part * n, (part + 1) * n)
+            value = jnp.where(live, jnp.concatenate([low[rows], high[rows]], axis=0), 0.0)
             start = pl.multiple_of((2 * k + part) * wide + at * sources, sources)
             rhs[k, pl.ds(start, sources), :] = value.astype(jnp.bfloat16)
             start = pl.multiple_of((2 * k + 1 - part) * wide + at * sources, sources)
@@ -336,9 +336,9 @@
     out_ref[...] = mix[...].astype(jnp.bfloat16)
 
 
-def bands_of(at_near, offsets, ranks, coeffs, u_own, groups, other=None):
+def bands_of(at_near, offsets, ranks, same, cross, u_own, groups, other=None):
     add = other is not None
-    freqs, _, sources, slots = coeffs.shape
+    freqs, sources, slots = same.shape
     tile = u_own.shape[2]
     rows = 2 * freqs * tile * 2 * sources // LANES // groups
     partial = jax.ShapeDtypeStruct((tile, LANES), jnp.float32)
@@ -347,7 +347,7 @@
     mixing = [pltpu.VMEM((tile, LANES), jnp.float32), pltpu.VMEM(whole.shape, jnp.float32)]
     return pl.pallas_call(
         functools.partial(band_kernel, add, at_near),
-        in_specs=[SMEM] * 2 + [VMEM] * (3 if add else 2),
+        in_specs=[SMEM] * 2 + [VMEM] * (4 if add else 3),
         out_specs=VMEM,
         out_shape=whole if add else partial,
         scratch_shapes=[spread, spread] + (mixing if add else []),
@@ -356,7 +356,7 @@
             flops=2 * 2 * freqs * tile * LANES * slots, bytes_accessed=2**20, transcendentals=0
         ),
         name="bands",
-    )(offsets, ranks, coeffs, u_own, *([other] if add else []))
+    )(offsets, ranks, same, cross, u_own, *([other] if add else []))
 
 
 def series_kernel(scale, bands_ref, table_ref, out_ref, wide, done, sems):
@@ -442,32 +442,38 @@
     freqs = freq_dev * groups
     sources = src_dev * row_group
     tile = u_factors.shape[3]
-    across = [(i, i ^ 2) for i in range(row_group)]
-    beside = [(i, i ^ 1) for i in range(row_group)]
+
+    def swapped(value, bits):
+        return lax.ppermute(value, "rows", [(i, i ^ bits) for i in range(row_group)])
+
+    twin, far, both = 1, 2, 3
     forward, _ = spectral_tables(freqs, samples)
     u_own, v_own = u_factors[:, :, 0], v_factors[:, :, 0]
-    v_far = lax.ppermute(v_own, "rows", across)
-    offsets_far = lax.ppermute(tile_offsets, "rows", across)
+    v_far = swapped(v_own, far)
+    v_twin = swapped(v_own, twin)
     table = forward.reshape(2 * freqs, samples)
+    offsets = [tile_offsets] + [swapped(tile_offsets, bits) for bits in (twin, far, both)]
     sent = transform(wavefield.reshape(rec_dev * src_dev, samples), table, groups)
-    own = {0: sent[0]}
+    blocks = {0: sent[0]}
     for shift in shift_order(groups):
         swap = [(i, i ^ shift) for i in range(groups)]
-        own[shift] = lax.ppermute(sent[shift], "freq", swap)
+        blocks[shift] = lax.ppermute(sent[shift], "freq", swap)
     early, late = arrivals(groups)
-    own_early, own_late = [own[s] for s in early], [own[s] for s in late]
-    twin_early = []
-    for shift, block in zip(early, own_early):
-        twin_early.append(lax.ppermute(block, "rows", beside))
-    (near,) = coefficients(early, [tile_offsets], own_early, twin_early, [v_own])
-    (leaving,) = coefficients(early, [offsets_far], own_early, twin_early, [v_far])
-    own_late, near, leaving = lax.optimization_barrier((own_late, near, leaving))
-    twin_late = [lax.ppermute(block, "rows", beside) for block in own_late]
-    (leaving,) = coefficients(late, [offsets_far], own_late, twin_late, [v_far], [leaving])
-    far = lax.ppermute(leaving, "rows", across)
-    (near,) = coefficients(late, [tile_offsets], own_late, twin_late, [v_own], [near])
-    half = bands_of(True, tile_offsets, tile_ranks, near, u_own, groups)
-    bands = bands_of(False, tile_offsets, tile_ranks, far, u_own, groups, half)
+    soon, later = [blocks[s] for s in early], [blocks[s] for s in late]
+    own, to_twin = coefficients(early, offsets[:2], soon, [v_own, v_twin])
+    v_far, own, to_twin = lax.optimization_barrier((v_far, own, to_twin))
+    v_both = swapped(v_far, twin)
+    (to_far,) = coefficients(early, offsets[2:3], soon, [v_far])
+    v_both, to_far = lax.optimization_barrier((v_both, to_far))
+    (to_both,) = coefficients(early, offsets[3:], soon, [v_both])
+    later, to_both, to_far = lax.optimization_barrier((later, to_both, to_far))
+    to_far, to_both = coefficients(late, offsets[2:], later, [v_far, v_both], [to_far, to_both])
+    later, to_far, to_both = lax.optimization_barrier((later, to_far, to_both))
+    from_far, from_both = swapped(to_far, far), swapped(to_both, both)
+    own, to_twin = coefficients(late, offsets[:2], later, [v_own, v_twin], [own, to_twin])
+    from_twin = swapped(to_twin, twin)
+    half = bands_of(True, tile_offsets, tile_ranks, own, from_twin, u_own, groups)
+    bands = bands_of(False, tile_offsets, tile_ranks, from_far, from_both, u_own, groups, half)
     returned = lax.all_to_all(bands, "freq", split_axis=0, concat_axis=0, tiled=True)
     series = series_of(returned, table, math.sqrt(samples) / math.sqrt(freqs))
     return series.reshape(tile // groups, sources, samples)

time: 59 us -> 64.6 us (1.095)
  Pallas kernels: 19.1 us -> 21.9 us
  waiting for transfers between devices: 8.98 us -> 11.7 us
  starting transfers between devices: 18.6 us -> 17.4 us
  blocking collectives: 11.5 us -> 12.7 us
    pallas_call x4 -> x5, Pallas kernels: 5.73 us -> 8.48 us  [coefficients(): pl.pallas_call(functools.partial(coefficient_kernel, tuple(shifts), sides...]
    ppermute x18 -> x16, waiting for transfers between devices: 8.98 us -> 11.7 us  [the longest x7 9.1 us: per_device_fast(): blocks[shift] = lax.ppermute(sent[shift], 'freq', swap)]
    ppermute x18 -> x16, starting transfers between devices: 18.6 us -> 17.4 us  [the longest x7 10.5 us: per_device_fast(): blocks[shift] = lax.ppermute(sent[shift], 'freq', swap)]
    all_to_all x1, blocking collectives: 11.5 us -> 12.7 us  [per_device_fast(): lax.all_to_all(bands, 'freq', split_axis=0, concat_axis=0, tiled=True)]
  transfers between devices with their start and end apart: 18 -> 16, of which waited for: 9 -> 8; matrix products, arithmetic and copies ran while one was open for 1% -> 1% of each run, Pallas kernels for 26% -> 24%
where the time goes in v1:
time: 64.6 us; the launch traced here: 64.4 us
  Pallas kernels  21.9 us (34%)
  starting transfers between devices  17.4 us (27%)
  blocking collectives  12.7 us (20%)
  waiting for transfers between devices  11.7 us (18%)
    all_to_all x1, blocking collectives, per_device_fast(): lax.all_to_all(bands, 'freq', split_axis=0, concat_axis=0, tiled=True)  12.7 us
    ppermute x7, starting transfers between devices, per_device_fast(): blocks[shift] = lax.ppermute(sent[shift], 'freq', swap)  10.5 us
    pallas_call x1, Pallas kernels, transform(): pl.pallas_call(transform_kernel, in_specs=[pl.BlockSpec(memory_space=pltp...  9.66 us
    ppermute x7, waiting for transfers between devices, per_device_fast(): blocks[shift] = lax.ppermute(sent[shift], 'freq', swap)  9.1 us
    pallas_call x5, Pallas kernels, coefficients(): pl.pallas_call(functools.partial(coefficient_kernel, tuple(shifts), sides...  8.48 us
    ppermute x9, starting transfers between devices, swapped(): lax.ppermute(value, 'rows', [(i, i ^ bits) for i in range(row_group)])  6.89 us
    ppermute x9, waiting for transfers between devices, swapped(): lax.ppermute(value, 'rows', [(i, i ^ bits) for i in range(row_group)])  2.62 us
    pallas_call x2, Pallas kernels, bands_of(): pl.pallas_call(functools.partial(band_kernel, add, at_near), in_specs=[SM...  2.14 us
  transfers between devices with their start and end apart: 16, of which 8 were waited for; matrix products, arithmetic and copies ran while one was open for 1% of the time, Pallas kernels for 24%

profile of v1, /device:TPU:0, one launch (start us, length us, event | category | flops | bytes accessed | tf_op | source)
XLA Modules:
  0.0 64.4 jit_solution(5471832460613021134)
XLA Ops:
  0.0 0.5 collective-permute-start.10
  0.5 2.5 %collective-permute-start.8 = (bf16[2,2,512,256]{3,2,1,0:T(8,128)(2,1)}, bf16[2,2,512,256]{3,2,1,0:T(8,128)(2,1)}, u32[]{:S(2)}, u32[]{:S(2)}) collective-permute-start(bf16[2,2,512,256]{3,2,1,0:T(8,128)(2,1)} %bitcast.9), channel_id=1, source_target_pairs={{0,2},{1,3},{2,0},{3,1},{4,6},{5,7},{6,4},{7,5},{8,10},{9,11},{10,... | collective-permute-start | bytes 3145736 | tf_op jit(solution)/shard_map/ppermute | solution.py:447
  3.0 0.3 fusion.7
  3.6 9.7 %transform.1 = (bf16[32,1280]{1,0:T(8,128)(2,1)S(1)}, bf16[32,1280]{1,0:T(8,128)(2,1)S(1)}, bf16[32,1280]{1,0:T(8,128)(2,1)S(1)}, bf16[32,1280]{1,0:T(8,128)(2,1...) custom-call(bf16[10240,1024]{1,0:T(8,128)(2,1)} %bitcast.12, ...), custom_call_target="tpu_custom_call" | custom-call | flops 5368709120 | bytes 20971520 | tf_op jit(solution)/shard_map/transform/pallas_call | solution.py:186
  13.3 2.7 %collective-permute-start.3 = (bf16[32,1280]{1,0:T(8,128)(2,1)S(1)}, bf16[32,1280]{1,0:T(8,128)(2,1)S(1)}, u32[]{:S(2)}, u32[]{:S(2)}) collective-permute-start(bf16[32,1280]{1,0:T(8,128)(2,1)S(1)} %get-tuple-element.35), channel_id=1, source_target_pairs={{0,16},{4,20},{8,24},{12,28},{16,0},{20,4},{24,8},{28,12},{1,17},{... | collective-permute-start | bytes 245768 | tf_op jit(solution)/shard_map/ppermute | solution.py:460
  15.9 1.6 %collective-permute-start.4 = (bf16[32,1280]{1,0:T(8,128)(2,1)S(1)}, bf16[32,1280]{1,0:T(8,128)(2,1)S(1)}, u32[]{:S(2)}, u32[]{:S(2)}) collective-permute-start(bf16[32,1280]{1,0:T(8,128)(2,1)S(1)} %get-tuple-element.36), channel_id=1, source_target_pairs={{0,8},{4,12},{8,0},{12,4},{16,24},{20,28},{24,16},{28,20},{1,9},{5... | collective-permute-start | bytes 245768 | tf_op jit(solution)/shard_map/ppermute | solution.py:460
  17.5 1.2 %collective-permute-done.9.refs_1_ = s32[2,1,40]{2,1,0:T(1,128)S(1)} collective-permute-done((s32[2,1,40]{2,1,0:T(1,128)S(1)}, s32[2,1,40]{2,1,0:T(1,128)S(1)}, u32[]{:S(2)}, u32[]{:S(2)}) %collective-permute-start.9) | collective-permute-done | bytes 352 | tf_op jit(solution)/shard_map/ppermute | solution.py:447
  18.6 1.2 %collective-permute-start.5 = (bf16[32,1280]{1,0:T(8,128)(2,1)S(1)}, bf16[32,1280]{1,0:T(8,128)(2,1)S(1)}, u32[]{:S(2)}, u32[]{:S(2)}) collective-permute-start(bf16[32,1280]{1,0:T(8,128)(2,1)S(1)} %get-tuple-element.37), channel_id=1, source_target_pairs={{0,28},{4,24},{8,20},{12,16},{16,12},{20,8},{24,4},{28,0},{1,29},{... | collective-permute-start | bytes 245768 | tf_op jit(solution)/shard_map/ppermute | solution.py:460
  19.8 0.6 collective-permute-done.3.refs_3_.refs_2_
  20.4 2.0 %collective-permute-start.6 = (bf16[32,1280]{1,0:T(8,128)(2,1)S(1)}, bf16[32,1280]{1,0:T(8,128)(2,1)S(1)}, u32[]{:S(2)}, u32[]{:S(2)}) collective-permute-start(bf16[32,1280]{1,0:T(8,128)(2,1)S(1)} %get-tuple-element.38), channel_id=1, source_target_pairs={{0,12},{4,8},{8,4},{12,0},{16,28},{20,24},{24,20},{28,16},{1,13},{... | collective-permute-start | bytes 245768 | tf_op jit(solution)/shard_map/ppermute | solution.py:460
  22.4 0.3 collective-permute-start.7
  22.7 3.4 %collective-permute-done.5.refs_5_.refs_4_ = bf16[32,1280]{1,0:T(8,128)(2,1)S(1)} collective-permute-done((bf16[32,1280]{1,0:T(8,128)(2,1)S(1)}, bf16[32,1280]{1,0:T(8,128)(2,1)S(1)}, u32[]{:S(2)}, u32[]{:S(2)}) %collective-permute-start.5) | collective-permute-done | bytes 81952 | tf_op jit(solution)/shard_map/ppermute | solution.py:460
  26.0 0.8 %collective-permute-done.6.refs_6_.refs_5_ = bf16[32,1280]{1,0:T(8,128)(2,1)S(1)} collective-permute-done((bf16[32,1280]{1,0:T(8,128)(2,1)S(1)}, bf16[32,1280]{1,0:T(8,128)(2,1)S(1)}, u32[]{:S(2)}, u32[]{:S(2)}) %collective-permute-start.6) | collective-permute-done | bytes 81952 | tf_op jit(solution)/shard_map/ppermute | solution.py:460
  26.8 1.7 %collective-permute-done.7.refs_7_.refs_6_ = bf16[32,1280]{1,0:T(8,128)(2,1)S(1)} collective-permute-done((bf16[32,1280]{1,0:T(8,128)(2,1)S(1)}, bf16[32,1280]{1,0:T(8,128)(2,1)S(1)}, u32[]{:S(2)}, u32[]{:S(2)}) %collective-permute-start.7) | collective-permute-done | bytes 81952 | tf_op jit(solution)/shard_map/ppermute | solution.py:460
  28.5 1.8 %coefficients.5 = (bf16[2,16,512]{2,1,0:T(8,128)(2,1)S(1)}, bf16[2,16,512]{2,1,0:T(8,128)(2,1)S(1)}) custom-call(s32[2,1,40]{2,1,0:T(1,128)S(1)} %copy-done.1, s32[2,1,40]{2,1,0:T(1,128)S(1)} %collective-permute-done.9.refs_1_, bf16[32,1280]{1,0:T(8,128)(2,1)S(1)} %get-tuple-element.34.refs_2_.refs_1_, ...), custom_call_target="tpu_custom_call" | custom-call | flops 2013265920 | bytes 1048576 | tf_op jit(solution)/shard_map/coefficients/pallas_call | solution.py:271
  30.4 0.6 collective-permute-start.12
  31.0 1.2 %collective-permute-start.2 = (s32[2,1,40]{2,1,0:T(1,128)S(1)}, s32[2,1,40]{2,1,0:T(1,128)S(1)}, u32[]{:S(2)}, u32[]{:S(2)}) collective-permute-start(s32[2,1,40]{2,1,0:T(1,128)S(1)} %copy-done.1), channel_id=1, source_target_pairs={{0,3},{1,2},{2,1},{3,0},{4,7},{5,6},{6,5},{7,4},{8,11},{9,10},{10,... | collective-permute-start | bytes 968 | tf_op jit(solution)/shard_map/ppermute | solution.py:447
  32.2 2.5 %collective-permute-start = (bf16[32,1280]{1,0:T(8,128)(2,1)S(1)}, bf16[32,1280]{1,0:T(8,128)(2,1)S(1)}, u32[]{:S(2)}, u32[]{:S(2)}) collective-permute-start(bf16[32,1280]{1,0:T(8,128)(2,1)S(1)} %get-tuple-element.32), channel_id=1, source_target_pairs={{0,20},{4,16},{8,28},{12,24},{16,4},{20,0},{24,12},{28,8},{1,21},{... | collective-permute-start | bytes 245768 | tf_op jit(solution)/shard_map/ppermute | solution.py:460
  34.7 0.4 collective-permute-start.1
  35.1 1.9 %coefficients.6.refs_6_ = bf16[2,16,512]{2,1,0:T(8,128)(2,1)S(1)} custom-call(s32[2,1,40]{2,1,0:T(1,128)S(1)} %collective-permute-done.12.refs_0_, bf16[32,1280]{1,0:T(8,128)(2,1)S(1)} %get-tuple-element.34.refs_2_.refs_1_, bf16[32,1280]{1,0:T(8,128)(2,1)S(1)} %collective-permute-done.3.refs_3_.refs_2_, ...), custom_call_target="tpu_custom_call" | custom-call | flops 1006632960 | bytes 1048576 | tf_op jit(solution)/shard_map/coefficients/pallas_call | solution.py:271
  37.0 1.3 %coefficients.7.refs_7_ = bf16[2,16,512]{2,1,0:T(8,128)(2,1)S(1)} custom-call(s32[2,1,40]{2,1,0:T(1,128)S(1)} %collective-permute-done.2.refs_0_.refs_1_, bf16[32,1280]{1,0:T(8,128)(2,1)S(1)} %get-tuple-element.34.refs_2_.refs_1_, bf16[32,1280]{1,0:T(8,128)(2,1)S(1)} %collective-permute-done.3.refs_3_.refs_2_, ...), custom_call_target="tpu_custom_call" | custom-call | flops 1006632960 | bytes 1048576 | tf_op jit(solution)/shard_map/coefficients/pallas_call | solution.py:271
  38.3 1.7 %collective-permute-done.refs_2_ = bf16[32,1280]{1,0:T(8,128)(2,1)S(1)} collective-permute-done((bf16[32,1280]{1,0:T(8,128)(2,1)S(1)}, bf16[32,1280]{1,0:T(8,128)(2,1)S(1)}, u32[]{:S(2)}, u32[]{:S(2)}) %collective-permute-start) | collective-permute-done | bytes 81952 | tf_op jit(solution)/shard_map/ppermute | solution.py:460
  40.0 1.1 %collective-permute-done.1.refs_3_ = bf16[32,1280]{1,0:T(8,128)(2,1)S(1)} collective-permute-done((bf16[32,1280]{1,0:T(8,128)(2,1)S(1)}, bf16[32,1280]{1,0:T(8,128)(2,1)S(1)}, u32[]{:S(2)}, u32[]{:S(2)}) %collective-permute-start.1) | collective-permute-done | bytes 81952 | tf_op jit(solution)/shard_map/ppermute | solution.py:460
  41.0 2.1 %coefficients.8 = (bf16[2,16,512]{2,1,0:T(8,128)(2,1)S(1)}, bf16[2,16,512]{2,1,0:T(8,128)(2,1)S(1)}) custom-call(s32[2,1,40]{2,1,0:T(1,128)S(1)} %collective-permute-done.12.refs_0_, s32[2,1,40]{2,1,0:T(1,128)S(1)} %collective-permute-done.2.refs_0_.refs_1_, bf16[32,1280]{1,0:T(8,128)(2,1)S(1)} %collective-permute-done.refs_2_, ...), custom_call_target="tpu_custom_call" | custom-call | flops 671088640 | bytes 1048576 | tf_op jit(solution)/shard_map/coefficients/pallas_call | solution.py:271
  43.1 1.4 %coefficients.9 = (bf16[2,16,512]{2,1,0:T(8,128)(2,1)S(1)}, bf16[2,16,512]{2,1,0:T(8,128)(2,1)S(1)}) custom-call(s32[2,1,40]{2,1,0:T(1,128)S(1)} %copy-done.1, s32[2,1,40]{2,1,0:T(1,128)S(1)} %collective-permute-done.9.refs_1_, bf16[32,1280]{1,0:T(8,128)(2,1)S(1)} %collective-permute-done.refs_2_, bf16[32,1280]{1,0:T(8,128)(2,1)S(1)} %collective-permute-done.1.refs_3_, ...), custom_call_target="tpu_custom_call" | custom-call | flops 671088640 | bytes 1048576 | tf_op jit(solution)/shard_map/coefficients/pallas_call | solution.py:271
  44.6 0.6 collective-permute-start.13
  45.3 1.2 %collective-permute-start.14 = (bf16[2,16,512]{2,1,0:T(8,128)(2,1)S(1)}, bf16[2,16,512]{2,1,0:T(8,128)(2,1)S(1)}, u32[]{:S(2)}, u32[]{:S(2)}) collective-permute-start(bf16[2,16,512]{2,1,0:T(8,128)(2,1)S(1)} %get-tuple-element.52), channel_id=1, source_target_pairs={{0,3},{1,2},{2,1},{3,0},{4,7},{5,6},{6,5},{7,4},{8,11},{9,10},{10,... | collective-permute-start | bytes 98312 | tf_op jit(solution)/shard_map/ppermute | solution.py:447
  46.5 1.0 %bands.2.refs_0_ = f32[256,128]{1,0:T(8,128)S(1)} custom-call(s32[2,1,40]{2,1,0:T(1,128)S(1)} %copy-done.1, s32[2,1,40]{2,1,0:T(1,128)S(1)} %copy-done.2, bf16[2,16,512]{2,1,0:T(8,128)(2,1)S(1)} %get-tuple-element.57.same_ref, bf16[2,16,512]{2,1,0:T(8,128)(2,1)S(1)} %collective-permute-done.15.cross_ref, bf16[2,2,256,512]{3,2,1,0:T(8,128)(2,1)S(1)} %bitcast.5), custom_call_target="tpu_custom_call" | custom-call | flops 134217728 | bytes 1048576 | tf_op jit(solution)/shard_map/bands/pallas_call | solution.py:348
  47.5 1.4 %collective-permute-done.13.same_ref = bf16[2,16,512]{2,1,0:T(8,128)(2,1)S(1)} collective-permute-done((bf16[2,16,512]{2,1,0:T(8,128)(2,1)S(1)}, bf16[2,16,512]{2,1,0:T(8,128)(2,1)S(1)}, u32[]{:S(2)}, u32[]{:S(2)}) %collective-permute-start.13) | collective-permute-done | bytes 32800 | tf_op jit(solution)/shard_map/ppermute | solution.py:447
  48.9 1.1 %bands.3 = bf16[8,32,128]{2,1,0:T(8,128)(2,1)S(1)} custom-call(s32[2,1,40]{2,1,0:T(1,128)S(1)} %copy-done.1, s32[2,1,40]{2,1,0:T(1,128)S(1)} %copy-done.2, bf16[2,16,512]{2,1,0:T(8,128)(2,1)S(1)} %collective-permute-done.13.same_ref, bf16[2,16,512]{2,1,0:T(8,128)(2,1)S(1)} %collective-permute-done.14.cross_ref, bf16[2,2,256,512]{3,2,1,0:T(8,128)(2,1)S(1)} %bitcast.6, ...), custom_call_target="tpu_custom_call" | custom-call | flops 134217728 | bytes 1048576 | tf_op jit(solution)/shard_map/bands/pallas_call | solution.py:348
  50.1 12.7 %all_to_all.5.bands_ref = bf16[8,32,128]{2,1,0:T(8,128)(2,1)S(1)} all-to-all(bf16[8,32,128]{2,1,0:T(8,128)(2,1)S(1)} %bands.3), channel_id=1, replica_groups=mesh['freq'=8,'rows'=4] {'freq'}, dimensions={0} | all-to-all | bytes 131072 | tf_op jit(solution)/shard_map/all_to_all | solution.py:477
  62.7 1.7 %series.1 = bf16[1024,1024]{1,0:T(8,128)(2,1)} custom-call(bf16[8,32,128]{2,1,0:T(8,128)(2,1)S(1)} %all_to_all.5.bands_ref, bf16[32,1024]{1,0:T(8,128)(2,1)S(1)} %convert_element_type.29.table_ref), custom_call_target="tpu_custom_call" | custom-call | flops 67108864 | bytes 2097152 | tf_op jit(solution)/shard_map/series/pallas_call | solution.py:387
  (24 shorter events, 0.3 us)
Async XLA Ops:
  0.0 28.5 %copy-start.3 = (bf16[2,2,1,512,256]{4,3,2,1,0:T(8,128)(2,1)S(1)}, bf16[2,2,1,512,256]{4,3,2,1,0:T(8,128)(2,1)}, u32[]{:S(2)}) copy-start(bf16[2,2,1,512,256]{4,3,2,1,0:T(8,128)(2,1)} %param.7) | copy-start | bytes 3145732
  0.0 17.5 %copy-start.1 = (s32[2,1,40]{2,1,0:T(1,128)S(1)}, s32[2,1,40]{2,1,0:T(1,128)}, u32[]{:S(2)}) copy-start(s32[2,1,40]{2,1,0:T(1,128)} %offsets_ref.3) | copy-start | bytes 964
  0.0 28.5 %collective-permute-start.10 = (bf16[2,2,512,256]{3,2,1,0:T(8,128)(2,1)}, bf16[2,2,512,256]{3,2,1,0:T(8,128)(2,1)S(1)}, u32[]{:S(2)}, u32[]{:S(2)}) collective-permute-start(bf16[2,2,512,256]{3,2,1,0:T(8,128)(2,1)} %bitcast.8), channel_id=1, source_target_pairs={{0,1},{1,0},{2,3},{3,2},{4,5},{5,4},{6,7},{7,6},{8,9},{9,8},{10,11... | collective-permute-start | bytes 3145736 | tf_op jit(solution)/shard_map/ppermute | solution.py:447
  0.5 29.8 %collective-permute-start.8 = (bf16[2,2,512,256]{3,2,1,0:T(8,128)(2,1)}, bf16[2,2,512,256]{3,2,1,0:T(8,128)(2,1)}, u32[]{:S(2)}, u32[]{:S(2)}) collective-permute-start(bf16[2,2,512,256]{3,2,1,0:T(8,128)(2,1)} %bitcast.9), channel_id=1, source_target_pairs={{0,2},{1,3},{2,0},{3,1},{4,6},{5,7},{6,4},{7,5},{8,10},{9,11},{10,... | collective-permute-start | bytes 3145736 | tf_op jit(solution)/shard_map/ppermute | solution.py:447
  3.4 43.1 %copy-start = (bf16[2,2,1,256,512]{4,3,2,1,0:T(8,128)(2,1)S(1)}, bf16[2,2,1,256,512]{4,3,2,1,0:T(8,128)(2,1)}, u32[]{:S(2)}) copy-start(bf16[2,2,1,256,512]{4,3,2,1,0:T(8,128)(2,1)} %param.6) | copy-start | bytes 3145732
  3.4 43.1 %copy-start.2 = (s32[2,1,40]{2,1,0:T(1,128)S(1)}, s32[2,1,40]{2,1,0:T(1,128)}, u32[]{:S(2)}) copy-start(s32[2,1,40]{2,1,0:T(1,128)} %ranks_ref.3) | copy-start | bytes 964
  13.3 7.1 %collective-permute-start.3 = (bf16[32,1280]{1,0:T(8,128)(2,1)S(1)}, bf16[32,1280]{1,0:T(8,128)(2,1)S(1)}, u32[]{:S(2)}, u32[]{:S(2)}) collective-permute-start(bf16[32,1280]{1,0:T(8,128)(2,1)S(1)} %get-tuple-element.35), channel_id=1, source_target_pairs={{0,16},{4,20},{8,24},{12,28},{16,0},{20,4},{24,8},{28,12},{1,17},{... | collective-permute-start | bytes 245768 | tf_op jit(solution)/shard_map/ppermute | solution.py:460
  15.9 6.5 %collective-permute-start.4 = (bf16[32,1280]{1,0:T(8,128)(2,1)S(1)}, bf16[32,1280]{1,0:T(8,128)(2,1)S(1)}, u32[]{:S(2)}, u32[]{:S(2)}) collective-permute-start(bf16[32,1280]{1,0:T(8,128)(2,1)S(1)} %get-tuple-element.36), channel_id=1, source_target_pairs={{0,8},{4,12},{8,0},{12,4},{16,24},{20,28},{24,16},{28,20},{1,9},{5... | collective-permute-start | bytes 245768 | tf_op jit(solution)/shard_map/ppermute | solution.py:460
  17.5 1.2 %collective-permute-start.9 = (s32[2,1,40]{2,1,0:T(1,128)S(1)}, s32[2,1,40]{2,1,0:T(1,128)S(1)}, u32[]{:S(2)}, u32[]{:S(2)}) collective-permute-start(s32[2,1,40]{2,1,0:T(1,128)S(1)} %copy-done.1), channel_id=1, source_target_pairs={{0,1},{1,0},{2,3},{3,2},{4,5},{5,4},{6,7},{7,6},{8,9},{9,8},{10,11... | collective-permute-start | bytes 968 | tf_op jit(solution)/shard_map/ppermute | solution.py:447
  18.6 7.4 %collective-permute-start.5 = (bf16[32,1280]{1,0:T(8,128)(2,1)S(1)}, bf16[32,1280]{1,0:T(8,128)(2,1)S(1)}, u32[]{:S(2)}, u32[]{:S(2)}) collective-permute-start(bf16[32,1280]{1,0:T(8,128)(2,1)S(1)} %get-tuple-element.37), channel_id=1, source_target_pairs={{0,28},{4,24},{8,20},{12,16},{16,12},{20,8},{24,4},{28,0},{1,29},{... | collective-permute-start | bytes 245768 | tf_op jit(solution)/shard_map/ppermute | solution.py:460
  20.4 6.4 %collective-permute-start.6 = (bf16[32,1280]{1,0:T(8,128)(2,1)S(1)}, bf16[32,1280]{1,0:T(8,128)(2,1)S(1)}, u32[]{:S(2)}, u32[]{:S(2)}) collective-permute-start(bf16[32,1280]{1,0:T(8,128)(2,1)S(1)} %get-tuple-element.38), channel_id=1, source_target_pairs={{0,12},{4,8},{8,4},{12,0},{16,28},{20,24},{24,20},{28,16},{1,13},{... | collective-permute-start | bytes 245768 | tf_op jit(solution)/shard_map/ppermute | solution.py:460
  22.4 6.1 %collective-permute-start.7 = (bf16[32,1280]{1,0:T(8,128)(2,1)S(1)}, bf16[32,1280]{1,0:T(8,128)(2,1)S(1)}, u32[]{:S(2)}, u32[]{:S(2)}) collective-permute-start(bf16[32,1280]{1,0:T(8,128)(2,1)S(1)} %get-tuple-element.39), channel_id=1, source_target_pairs={{0,4},{4,0},{8,12},{12,8},{16,20},{20,16},{24,28},{28,24},{1,5},{5... | collective-permute-start | bytes 245768 | tf_op jit(solution)/shard_map/ppermute | solution.py:460
  30.3 6.7 %collective-permute-start.11 = (bf16[2,2,512,256]{3,2,1,0:T(8,128)(2,1)}, bf16[2,2,512,256]{3,2,1,0:T(8,128)(2,1)S(1)}, u32[]{:S(2)}, u32[]{:S(2)}) collective-permute-start(bf16[2,2,512,256]{3,2,1,0:T(8,128)(2,1)} %collective-permute-done.8.refs_7_.refs_4_), channel_id=1, source_target_pairs={{0,1},{1,0},{2,3},{3,2},{4,5},{5,4},{6,7},{7,6},{8,9},{9,8},{10,11... | collective-permute-start | bytes 3145736 | tf_op jit(solution)/shard_map/ppermute | solution.py:447
  30.4 4.7 %collective-permute-start.12 = (s32[2,1,40]{2,1,0:T(1,128)S(1)}, s32[2,1,40]{2,1,0:T(1,128)S(1)}, u32[]{:S(2)}, u32[]{:S(2)}) collective-permute-start(s32[2,1,40]{2,1,0:T(1,128)S(1)} %copy-done.1), channel_id=1, source_target_pairs={{0,2},{1,3},{2,0},{3,1},{4,6},{5,7},{6,4},{7,5},{8,10},{9,11},{10,... | collective-permute-start | bytes 968 | tf_op jit(solution)/shard_map/ppermute | solution.py:447
  31.0 6.1 %collective-permute-start.2 = (s32[2,1,40]{2,1,0:T(1,128)S(1)}, s32[2,1,40]{2,1,0:T(1,128)S(1)}, u32[]{:S(2)}, u32[]{:S(2)}) collective-permute-start(s32[2,1,40]{2,1,0:T(1,128)S(1)} %copy-done.1), channel_id=1, source_target_pairs={{0,3},{1,2},{2,1},{3,0},{4,7},{5,6},{6,5},{7,4},{8,11},{9,10},{10,... | collective-permute-start | bytes 968 | tf_op jit(solution)/shard_map/ppermute | solution.py:447
  32.2 7.8 %collective-permute-start = (bf16[32,1280]{1,0:T(8,128)(2,1)S(1)}, bf16[32,1280]{1,0:T(8,128)(2,1)S(1)}, u32[]{:S(2)}, u32[]{:S(2)}) collective-permute-start(bf16[32,1280]{1,0:T(8,128)(2,1)S(1)} %get-tuple-element.32), channel_id=1, source_target_pairs={{0,20},{4,16},{8,28},{12,24},{16,4},{20,0},{24,12},{28,8},{1,21},{... | collective-permute-start | bytes 245768 | tf_op jit(solution)/shard_map/ppermute | solution.py:460
  34.7 6.3 %collective-permute-start.1 = (bf16[32,1280]{1,0:T(8,128)(2,1)S(1)}, bf16[32,1280]{1,0:T(8,128)(2,1)S(1)}, u32[]{:S(2)}, u32[]{:S(2)}) collective-permute-start(bf16[32,1280]{1,0:T(8,128)(2,1)S(1)} %get-tuple-element.33), channel_id=1, source_target_pairs={{0,24},{4,28},{8,16},{12,20},{16,8},{20,12},{24,0},{28,4},{1,25},{... | collective-permute-start | bytes 245768 | tf_op jit(solution)/shard_map/ppermute | solution.py:460
  44.5 1.9 %collective-permute-start.15 = (bf16[2,16,512]{2,1,0:T(8,128)(2,1)S(1)}, bf16[2,16,512]{2,1,0:T(8,128)(2,1)S(1)}, u32[]{:S(2)}, u32[]{:S(2)}) collective-permute-start(bf16[2,16,512]{2,1,0:T(8,128)(2,1)S(1)} %get-tuple-element.58), channel_id=1, source_target_pairs={{0,1},{1,0},{2,3},{3,2},{4,5},{5,4},{6,7},{7,6},{8,9},{9,8},{10,11... | collective-permute-start | bytes 98312 | tf_op jit(solution)/shard_map/ppermute | solution.py:447
  44.6 4.3 %collective-permute-start.13 = (bf16[2,16,512]{2,1,0:T(8,128)(2,1)S(1)}, bf16[2,16,512]{2,1,0:T(8,128)(2,1)S(1)}, u32[]{:S(2)}, u32[]{:S(2)}) collective-permute-start(bf16[2,16,512]{2,1,0:T(8,128)(2,1)S(1)} %get-tuple-element.51), channel_id=1, source_target_pairs={{0,2},{1,3},{2,0},{3,1},{4,6},{5,7},{6,4},{7,5},{8,10},{9,11},{10,... | collective-permute-start | bytes 98312 | tf_op jit(solution)/shard_map/ppermute | solution.py:447
  45.3 3.7 %collective-permute-start.14 = (bf16[2,16,512]{2,1,0:T(8,128)(2,1)S(1)}, bf16[2,16,512]{2,1,0:T(8,128)(2,1)S(1)}, u32[]{:S(2)}, u32[]{:S(2)}) collective-permute-start(bf16[2,16,512]{2,1,0:T(8,128)(2,1)S(1)} %get-tuple-element.52), channel_id=1, source_target_pairs={{0,3},{1,2},{2,1},{3,0},{4,7},{5,6},{6,5},{7,4},{8,11},{9,10},{10,... | collective-permute-start | bytes 98312 | tf_op jit(solution)/shard_map/ppermute | solution.py:447

commit v2 on v0

--- a/solution.py
+++ b/solution.py
@@ -15,7 +15,6 @@
 NT = (((1,), (1,)), ((), ()))
 VMEM = pl.BlockSpec(memory_space=pltpu.VMEM)
 SMEM = pl.BlockSpec(memory_space=pltpu.SMEM)
-LATE = 2
 PAIRED = (4, 8, 16)
 AHEAD = 3
 
@@ -430,8 +429,10 @@
 
 def arrivals(groups):
     order = shift_order(groups)
-    late = [s for s in order if s >= groups // 2][-LATE:]
-    return [0] + [s for s in order if s not in late], late
+    crossing = [s for s in order if s >= groups // 2]
+    middle = [s for s in order[:-1] if s == 1 or s in crossing[2:]]
+    early = [s for s in order[:-1] if s not in middle]
+    return [0] + early, middle, order[-1:]
 
 
 def per_device_fast(wavefield, u_factors, v_factors, tile_ranks, tile_offsets):
@@ -454,18 +455,30 @@
     for shift in shift_order(groups):
         swap = [(i, i ^ shift) for i in range(groups)]
         own[shift] = lax.ppermute(sent[shift], "freq", swap)
-    early, late = arrivals(groups)
-    own_early, own_late = [own[s] for s in early], [own[s] for s in late]
-    twin_early = []
-    for shift, block in zip(early, own_early):
-        twin_early.append(lax.ppermute(block, "rows", beside))
-    (near,) = coefficients(early, [tile_offsets], own_early, twin_early, [v_own])
-    (leaving,) = coefficients(early, [offsets_far], own_early, twin_early, [v_far])
-    own_late, near, leaving = lax.optimization_barrier((own_late, near, leaving))
-    twin_late = [lax.ppermute(block, "rows", beside) for block in own_late]
-    (leaving,) = coefficients(late, [offsets_far], own_late, twin_late, [v_far], [leaving])
+    early, middle, last = arrivals(groups)
+
+    def twins(shifts):
+        pairs = {}
+        for shift in shifts:
+            pairs[shift] = lax.ppermute(own[shift], "rows", beside)
+        return pairs
+
+    def blocks(shifts):
+        return [own[s] for s in shifts], [twin[s] for s in shifts]
+
+    twin = twins(early)
+    (near,) = coefficients(early, [tile_offsets], *blocks(early), [v_own])
+    waiting, near = lax.optimization_barrier(([own[s] for s in middle], near))
+    own.update(zip(middle, waiting))
+    twin.update(twins(middle))
+    (leaving,) = coefficients(early, [offsets_far], *blocks(early), [v_far])
+    waiting, near, leaving = lax.optimization_barrier(([own[s] for s in last], near, leaving))
+    own.update(zip(last, waiting))
+    twin.update(twins(last))
+    late = middle + last
+    (leaving,) = coefficients(late, [offsets_far], *blocks(late), [v_far], [leaving])
     far = lax.ppermute(leaving, "rows", across)
-    (near,) = coefficients(late, [tile_offsets], own_late, twin_late, [v_own], [near])
+    (near,) = coefficients(late, [tile_offsets], *blocks(late), [v_own], [near])
     half = bands_of(True, tile_offsets, tile_ranks, near, u_own, groups)
     bands = bands_of(False, tile_offsets, tile_ranks, far, u_own, groups, half)
     returned = lax.all_to_all(bands, "freq", split_axis=0, concat_axis=0, tiled=True)

time: 59 us -> 59 us (level)
  starting transfers between devices: 18.6 us -> 16.1 us
  waiting for transfers between devices: 8.98 us -> 11.2 us
    ppermute x1, starting transfers between devices: 1.42 us -> 0.07 us  [per_device_fast(): far = lax.ppermute(leaving, 'rows', across)]
    ppermute x1, waiting for transfers between devices: 0.87 us -> 1.94 us  [per_device_fast(): far = lax.ppermute(leaving, 'rows', across)]
    ppermute x7, starting transfers between devices: 12.3 us -> 11.3 us  [per_device_fast(): own[shift] = lax.ppermute(sent[shift], 'freq', swap)]
    ppermute x7, waiting for transfers between devices: 7.01 us -> 7.94 us  [per_device_fast(): own[shift] = lax.ppermute(sent[shift], 'freq', swap)]
  transfers between devices with their start and end apart: 18 -> 18, of which waited for: 9 -> 7; matrix products, arithmetic and copies ran while one was open for 1% -> 1% of each run, Pallas kernels for 26% -> 26%
where the time goes in v2:
time: 59 us; the launch traced here: 58.8 us
  Pallas kernels  19.1 us (32%)
  starting transfers between devices  16.1 us (27%)
  blocking collectives  11.8 us (20%)
  waiting for transfers between devices  11.2 us (19%)
    all_to_all x1, blocking collectives, per_device_fast(): lax.all_to_all(bands, 'freq', split_axis=0, concat_axis=0, tiled=True)  11.8 us
    ppermute x7, starting transfers between devices, per_device_fast(): own[shift] = lax.ppermute(sent[shift], 'freq', swap)  11.3 us
    pallas_call x1, Pallas kernels, transform(): pl.pallas_call(transform_kernel, in_specs=[pl.BlockSpec(memory_space=pltp...  9.56 us
    ppermute x7, waiting for transfers between devices, per_device_fast(): own[shift] = lax.ppermute(sent[shift], 'freq', swap)  7.94 us
    pallas_call x4, Pallas kernels, coefficients(): pl.pallas_call(functools.partial(coefficient_kernel, tuple(shifts), sides...  5.77 us
    ppermute x1, starting transfers between devices, per_device_fast(): v_far = lax.ppermute(v_own, 'rows', across)  3.04 us
    pallas_call x2, Pallas kernels, bands_of(): pl.pallas_call(functools.partial(band_kernel, add, at_near), in_specs=[SM...  2.13 us
    ppermute x1, waiting for transfers between devices, per_device_fast(): far = lax.ppermute(leaving, 'rows', across)  1.94 us
  transfers between devices with their start and end apart: 18, of which 7 were waited for; matrix products, arithmetic and copies ran while one was open for 1% of the time, Pallas kernels for 26%

profile of v2, /device:TPU:0, one launch (start us, length us, event | category | flops | bytes accessed | tf_op | source)
XLA Modules:
  0.0 58.8 jit_solution(460139908700863644)
XLA Ops:
  0.0 3.0 %collective-permute-start.13 = (bf16[2,2,512,256]{3,2,1,0:T(8,128)(2,1)}, bf16[2,2,512,256]{3,2,1,0:T(8,128)(2,1)S(1)}, u32[]{:S(2)}, u32[]{:S(2)}) collective-permute-start(bf16[2,2,512,256]{3,2,1,0:T(8,128)(2,1)} %bitcast.8), channel_id=1, source_target_pairs={{0,2},{1,3},{2,0},{3,1},{4,6},{5,7},{6,4},{7,5},{8,10},{9,11},{10,... | collective-permute-start | bytes 3145736 | tf_op jit(solution)/shard_map/ppermute | solution.py:450
  3.1 0.3 fusion.7
  3.4 0.1 copy.6
  3.6 9.6 %transform.1 = (bf16[32,1280]{1,0:T(8,128)(2,1)S(1)}, bf16[32,1280]{1,0:T(8,128)(2,1)S(1)}, bf16[32,1280]{1,0:T(8,128)(2,1)S(1)}, bf16[32,1280]{1,0:T(8,128)(2,1...) custom-call(bf16[10240,1024]{1,0:T(8,128)(2,1)} %bitcast.11, ...), custom_call_target="tpu_custom_call" | custom-call | flops 5368709120 | bytes 20971520 | tf_op jit(solution)/shard_map/transform/pallas_call | solution.py:185
  13.1 2.7 %collective-permute-start.3 = (bf16[32,1280]{1,0:T(8,128)(2,1)S(1)}, bf16[32,1280]{1,0:T(8,128)(2,1)S(1)}, u32[]{:S(2)}, u32[]{:S(2)}) collective-permute-start(bf16[32,1280]{1,0:T(8,128)(2,1)S(1)} %get-tuple-element.22), channel_id=1, source_target_pairs={{0,16},{4,20},{8,24},{12,28},{16,0},{20,4},{24,8},{28,12},{1,17},{... | collective-permute-start | bytes 245768 | tf_op jit(solution)/shard_map/ppermute | solution.py:457
  15.8 1.6 %collective-permute-start.4 = (bf16[32,1280]{1,0:T(8,128)(2,1)S(1)}, bf16[32,1280]{1,0:T(8,128)(2,1)S(1)}, u32[]{:S(2)}, u32[]{:S(2)}) collective-permute-start(bf16[32,1280]{1,0:T(8,128)(2,1)S(1)} %get-tuple-element.23), channel_id=1, source_target_pairs={{0,8},{4,12},{8,0},{12,4},{16,24},{20,28},{24,16},{28,20},{1,9},{5... | collective-permute-start | bytes 245768 | tf_op jit(solution)/shard_map/ppermute | solution.py:457
  17.4 1.2 %collective-permute-start.5 = (bf16[32,1280]{1,0:T(8,128)(2,1)S(1)}, bf16[32,1280]{1,0:T(8,128)(2,1)S(1)}, u32[]{:S(2)}, u32[]{:S(2)}) collective-permute-start(bf16[32,1280]{1,0:T(8,128)(2,1)S(1)} %get-tuple-element.24), channel_id=1, source_target_pairs={{0,28},{4,24},{8,20},{12,16},{16,12},{20,8},{24,4},{28,0},{1,29},{... | collective-permute-start | bytes 245768 | tf_op jit(solution)/shard_map/ppermute | solution.py:457
  18.5 0.6 %collective-permute-start.6 = (bf16[32,1280]{1,0:T(8,128)(2,1)S(1)}, bf16[32,1280]{1,0:T(8,128)(2,1)S(1)}, u32[]{:S(2)}, u32[]{:S(2)}) collective-permute-start(bf16[32,1280]{1,0:T(8,128)(2,1)S(1)} %get-tuple-element.25), channel_id=1, source_target_pairs={{0,12},{4,8},{8,4},{12,0},{16,28},{20,24},{24,20},{28,16},{1,13},{... | collective-permute-start | bytes 245768 | tf_op jit(solution)/shard_map/ppermute | solution.py:457
  19.2 0.1 collective-permute-done.3.refs_2_
  19.3 1.3 %collective-permute-done.4.refs_3_ = bf16[32,1280]{1,0:T(8,128)(2,1)S(1)} collective-permute-done((bf16[32,1280]{1,0:T(8,128)(2,1)S(1)}, bf16[32,1280]{1,0:T(8,128)(2,1)S(1)}, u32[]{:S(2)}, u32[]{:S(2)}) %collective-permute-start.4) | collective-permute-done | bytes 81952 | tf_op jit(solution)/shard_map/ppermute | solution.py:457
  20.7 4.0 %collective-permute-done.5.refs_4_ = bf16[32,1280]{1,0:T(8,128)(2,1)S(1)} collective-permute-done((bf16[32,1280]{1,0:T(8,128)(2,1)S(1)}, bf16[32,1280]{1,0:T(8,128)(2,1)S(1)}, u32[]{:S(2)}, u32[]{:S(2)}) %collective-permute-start.5) | collective-permute-done | bytes 81952 | tf_op jit(solution)/shard_map/ppermute | solution.py:457
  24.6 0.2 collective-permute-done.6.refs_5_
  24.9 0.3 collective-permute-start.10
  25.1 0.2 collective-permute-start.11
  25.4 2.6 %collective-permute-start.1 = (bf16[32,1280]{1,0:T(8,128)(2,1)S(1)}, bf16[32,1280]{1,0:T(8,128)(2,1)S(1)}, u32[]{:S(2)}, u32[]{:S(2)}) collective-permute-start(bf16[32,1280]{1,0:T(8,128)(2,1)S(1)} %get-tuple-element.19), channel_id=1, source_target_pairs={{0,20},{4,16},{8,28},{12,24},{16,4},{20,0},{24,12},{28,8},{1,21},{... | collective-permute-start | bytes 245768 | tf_op jit(solution)/shard_map/ppermute | solution.py:457
  28.0 1.1 %collective-permute-start.2 = (bf16[32,1280]{1,0:T(8,128)(2,1)S(1)}, bf16[32,1280]{1,0:T(8,128)(2,1)S(1)}, u32[]{:S(2)}, u32[]{:S(2)}) collective-permute-start(bf16[32,1280]{1,0:T(8,128)(2,1)S(1)} %get-tuple-element.20), channel_id=1, source_target_pairs={{0,4},{4,0},{8,12},{12,8},{16,20},{20,16},{24,28},{28,24},{1,5},{5... | collective-permute-start | bytes 245768 | tf_op jit(solution)/shard_map/ppermute | solution.py:457
  29.0 0.5 collective-permute-start
  29.6 1.7 %collective-permute-start.12 = (bf16[32,1280]{1,0:T(8,128)(2,1)S(1)}, bf16[32,1280]{1,0:T(8,128)(2,1)S(1)}, u32[]{:S(2)}, u32[]{:S(2)}) collective-permute-start(bf16[32,1280]{1,0:T(8,128)(2,1)S(1)} %get-tuple-element.28), channel_id=1, source_target_pairs={{0,24},{4,28},{8,16},{12,20},{16,8},{20,12},{24,0},{28,4},{1,25},{... | collective-permute-start | bytes 245768 | tf_op jit(solution)/shard_map/ppermute | solution.py:457
  31.2 1.6 %coefficients.4.refs_8_ = bf16[2,2,16,512]{3,2,1,0:T(8,128)(2,1)S(1)} custom-call(s32[2,1,40]{2,1,0:T(1,128)S(1)} %copy-done.1, bf16[32,1280]{1,0:T(8,128)(2,1)S(1)} %get-tuple-element.21.refs_1_, bf16[32,1280]{1,0:T(8,128)(2,1)S(1)} %collective-permute-done.3.refs_2_, bf16[32,1280]{1,0:T(8,128)(2,1)S(1)} %collective-permute-done.4.refs_3_, ...), custom_call_target="tpu_custom_call" | custom-call | flops 838860800 | bytes 1048576 | tf_op jit(solution)/shard_map/coefficients/pallas_call | solution.py:275
  32.9 2.3 %collective-permute-done.1.refs_1_ = bf16[32,1280]{1,0:T(8,128)(2,1)S(1)} collective-permute-done((bf16[32,1280]{1,0:T(8,128)(2,1)S(1)}, bf16[32,1280]{1,0:T(8,128)(2,1)S(1)}, u32[]{:S(2)}, u32[]{:S(2)}) %collective-permute-start.1) | collective-permute-done | bytes 81952 | tf_op jit(solution)/shard_map/ppermute | solution.py:457
  35.1 0.5 collective-permute-start.15
  35.6 1.6 %coefficients.5.refs_8_ = bf16[2,2,16,512]{3,2,1,0:T(8,128)(2,1)S(1)} custom-call(s32[2,1,40]{2,1,0:T(1,128)S(1)} %collective-permute-done.refs_0_, bf16[32,1280]{1,0:T(8,128)(2,1)S(1)} %get-tuple-element.21.refs_1_, bf16[32,1280]{1,0:T(8,128)(2,1)S(1)} %collective-permute-done.3.refs_2_, bf16[32,1280]{1,0:T(8,128)(2,1)S(1)} %collective-permute-done.4.refs_3_, ...), custom_call_target="tpu_custom_call" | custom-call | flops 838860800 | bytes 1048576 | tf_op jit(solution)/shard_map/coefficients/pallas_call | solution.py:275
  37.3 0.1 collective-permute-start.16
  37.4 1.2 %collective-permute-done.16.refs_6_ = bf16[32,1280]{1,0:T(8,128)(2,1)S(1)} collective-permute-done((bf16[32,1280]{1,0:T(8,128)(2,1)S(1)}, bf16[32,1280]{1,0:T(8,128)(2,1)S(1)}, u32[]{:S(2)}, u32[]{:S(2)}) %collective-permute-start.16) | collective-permute-done | bytes 81952 | tf_op jit(solution)/shard_map/ppermute | solution.py:463
  38.6 1.3 %coefficients.6 = bf16[2,2,16,512]{3,2,1,0:T(8,128)(2,1)S(1)} custom-call(s32[2,1,40]{2,1,0:T(1,128)S(1)} %collective-permute-done.refs_0_, bf16[32,1280]{1,0:T(8,128)(2,1)S(1)} %collective-permute-done.1.refs_1_, bf16[32,1280]{1,0:T(8,128)(2,1)S(1)} %collective-permute-done.2.refs_2_, bf16[32,1280]{1,0:T(8,128)(2,1)S(1)} %collective-permute-done.12.refs_3_, ...), custom_call_target="tpu_custom_call" | custom-call | flops 503316480 | bytes 1048576 | tf_op jit(solution)/shard_map/coefficients/pallas_call | solution.py:275
  39.9 0.1 collective-permute-start.17
  40.0 1.3 %coefficients.7.coeffs_ref = bf16[2,2,16,512]{3,2,1,0:T(8,128)(2,1)S(1)} custom-call(s32[2,1,40]{2,1,0:T(1,128)S(1)} %copy-done.1, bf16[32,1280]{1,0:T(8,128)(2,1)S(1)} %collective-permute-done.1.refs_1_, bf16[32,1280]{1,0:T(8,128)(2,1)S(1)} %collective-permute-done.2.refs_2_, bf16[32,1280]{1,0:T(8,128)(2,1)S(1)} %collective-permute-done.12.refs_3_, ...), custom_call_target="tpu_custom_call" | custom-call | flops 503316480 | bytes 1048576 | tf_op jit(solution)/shard_map/coefficients/pallas_call | solution.py:275
  41.3 1.0 %bands.2.refs_0_ = f32[256,128]{1,0:T(8,128)S(1)} custom-call(s32[2,1,40]{2,1,0:T(1,128)S(1)} %copy-done.1, s32[2,1,40]{2,1,0:T(1,128)S(1)} %copy-done.2, bf16[2,2,16,512]{3,2,1,0:T(8,128)(2,1)S(1)} %coefficients.7.coeffs_ref, bf16[2,2,256,512]{3,2,1,0:T(8,128)(2,1)S(1)} %bitcast.5), custom_call_target="tpu_custom_call" | custom-call | flops 134217728 | bytes 1048576 | tf_op jit(solution)/shard_map/bands/pallas_call | solution.py:347
  42.3 1.9 %collective-permute-done.17.coeffs_ref = bf16[2,2,16,512]{3,2,1,0:T(8,128)(2,1)S(1)} collective-permute-done((bf16[2,2,16,512]{3,2,1,0:T(8,128)(2,1)S(1)}, bf16[2,2,16,512]{3,2,1,0:T(8,128)(2,1)S(1)}, u32[]{:S(2)}, u32[]{:S(2)}) %collective-permute-start.17) | collective-permute-done | bytes 65568 | tf_op jit(solution)/shard_map/ppermute | solution.py:480
  44.2 1.1 %bands.3 = bf16[8,32,128]{2,1,0:T(8,128)(2,1)S(1)} custom-call(s32[2,1,40]{2,1,0:T(1,128)S(1)} %copy-done.1, s32[2,1,40]{2,1,0:T(1,128)S(1)} %copy-done.2, bf16[2,2,16,512]{3,2,1,0:T(8,128)(2,1)S(1)} %collective-permute-done.17.coeffs_ref, bf16[2,2,256,512]{3,2,1,0:T(8,128)(2,1)S(1)} %bitcast.6, f32[256,128]{1,0:T(8,128)S(1)} %bands.2.refs_0_), custom_call_target="tpu_custom_call" | custom-call | flops 134217728 | bytes 1048576 | tf_op jit(solution)/shard_map/bands/pallas_call | solution.py:347
  45.4 11.8 %all_to_all.5.bands_ref = bf16[8,32,128]{2,1,0:T(8,128)(2,1)S(1)} all-to-all(bf16[8,32,128]{2,1,0:T(8,128)(2,1)S(1)} %bands.3), channel_id=1, replica_groups=mesh['freq'=8,'rows'=4] {'freq'}, dimensions={0} | all-to-all | bytes 131072 | tf_op jit(solution)/shard_map/all_to_all | solution.py:484
  57.2 1.7 %series.1 = bf16[1024,1024]{1,0:T(8,128)(2,1)} custom-call(bf16[8,32,128]{2,1,0:T(8,128)(2,1)S(1)} %all_to_all.5.bands_ref, bf16[32,1024]{1,0:T(8,128)(2,1)S(1)} %convert_element_type.29.table_ref), custom_call_target="tpu_custom_call" | custom-call | flops 67108864 | bytes 2097152 | tf_op jit(solution)/shard_map/series/pallas_call | solution.py:386
  (27 shorter events, 0.1 us)
Async XLA Ops:
  0.0 31.2 %copy-start.3 = (bf16[2,2,1,512,256]{4,3,2,1,0:T(8,128)(2,1)S(1)}, bf16[2,2,1,512,256]{4,3,2,1,0:T(8,128)(2,1)}, u32[]{:S(2)}) copy-start(bf16[2,2,1,512,256]{4,3,2,1,0:T(8,128)(2,1)} %param.7) | copy-start | bytes 3145732
  0.0 29.0 %copy-start.1 = (s32[2,1,40]{2,1,0:T(1,128)S(1)}, s32[2,1,40]{2,1,0:T(1,128)}, u32[]{:S(2)}) copy-start(s32[2,1,40]{2,1,0:T(1,128)} %offsets_ref.3) | copy-start | bytes 964
  0.0 41.3 %copy-start.2 = (s32[2,1,40]{2,1,0:T(1,128)S(1)}, s32[2,1,40]{2,1,0:T(1,128)}, u32[]{:S(2)}) copy-start(s32[2,1,40]{2,1,0:T(1,128)} %ranks_ref.3) | copy-start | bytes 964
  0.0 41.3 %copy-start = (bf16[2,2,1,256,512]{4,3,2,1,0:T(8,128)(2,1)S(1)}, bf16[2,2,1,256,512]{4,3,2,1,0:T(8,128)(2,1)}, u32[]{:S(2)}) copy-start(bf16[2,2,1,256,512]{4,3,2,1,0:T(8,128)(2,1)} %param.6) | copy-start | bytes 3145732
  0.0 35.6 %collective-permute-start.13 = (bf16[2,2,512,256]{3,2,1,0:T(8,128)(2,1)}, bf16[2,2,512,256]{3,2,1,0:T(8,128)(2,1)S(1)}, u32[]{:S(2)}, u32[]{:S(2)}) collective-permute-start(bf16[2,2,512,256]{3,2,1,0:T(8,128)(2,1)} %bitcast.8), channel_id=1, source_target_pairs={{0,2},{1,3},{2,0},{3,1},{4,6},{5,7},{6,4},{7,5},{8,10},{9,11},{10,... | collective-permute-start | bytes 3145736 | tf_op jit(solution)/shard_map/ppermute | solution.py:450
  13.1 6.2 %collective-permute-start.3 = (bf16[32,1280]{1,0:T(8,128)(2,1)S(1)}, bf16[32,1280]{1,0:T(8,128)(2,1)S(1)}, u32[]{:S(2)}, u32[]{:S(2)}) collective-permute-start(bf16[32,1280]{1,0:T(8,128)(2,1)S(1)} %get-tuple-element.22), channel_id=1, source_target_pairs={{0,16},{4,20},{8,24},{12,28},{16,0},{20,4},{24,8},{28,12},{1,17},{... | collective-permute-start | bytes 245768 | tf_op jit(solution)/shard_map/ppermute | solution.py:457
  15.8 4.9 %collective-permute-start.4 = (bf16[32,1280]{1,0:T(8,128)(2,1)S(1)}, bf16[32,1280]{1,0:T(8,128)(2,1)S(1)}, u32[]{:S(2)}, u32[]{:S(2)}) collective-permute-start(bf16[32,1280]{1,0:T(8,128)(2,1)S(1)} %get-tuple-element.23), channel_id=1, source_target_pairs={{0,8},{4,12},{8,0},{12,4},{16,24},{20,28},{24,16},{28,20},{1,9},{5... | collective-permute-start | bytes 245768 | tf_op jit(solution)/shard_map/ppermute | solution.py:457
  17.4 7.2 %collective-permute-start.5 = (bf16[32,1280]{1,0:T(8,128)(2,1)S(1)}, bf16[32,1280]{1,0:T(8,128)(2,1)S(1)}, u32[]{:S(2)}, u32[]{:S(2)}) collective-permute-start(bf16[32,1280]{1,0:T(8,128)(2,1)S(1)} %get-tuple-element.24), channel_id=1, source_target_pairs={{0,28},{4,24},{8,20},{12,16},{16,12},{20,8},{24,4},{28,0},{1,29},{... | collective-permute-start | bytes 245768 | tf_op jit(solution)/shard_map/ppermute | solution.py:457
  18.5 6.3 %collective-permute-start.6 = (bf16[32,1280]{1,0:T(8,128)(2,1)S(1)}, bf16[32,1280]{1,0:T(8,128)(2,1)S(1)}, u32[]{:S(2)}, u32[]{:S(2)}) collective-permute-start(bf16[32,1280]{1,0:T(8,128)(2,1)S(1)} %get-tuple-element.25), channel_id=1, source_target_pairs={{0,12},{4,8},{8,4},{12,0},{16,28},{20,24},{24,20},{28,16},{1,13},{... | collective-permute-start | bytes 245768 | tf_op jit(solution)/shard_map/ppermute | solution.py:457
  19.3 5.8 %collective-permute-start.7 = (bf16[32,1280]{1,0:T(8,128)(2,1)S(1)}, bf16[32,1280]{1,0:T(8,128)(2,1)S(1)}, u32[]{:S(2)}, u32[]{:S(2)}) collective-permute-start(bf16[32,1280]{1,0:T(8,128)(2,1)S(1)} %get-tuple-element.21.refs_1_), channel_id=1, source_target_pairs={{0,1},{1,0},{2,3},{3,2},{4,5},{5,4},{6,7},{7,6},{8,9},{9,8},{10,11... | collective-permute-start | bytes 245768 | tf_op jit(solution)/shard_map/ppermute | solution.py:463
  20.7 4.7 %collective-permute-start.8 = (bf16[32,1280]{1,0:T(8,128)(2,1)S(1)}, bf16[32,1280]{1,0:T(8,128)(2,1)S(1)}, u32[]{:S(2)}, u32[]{:S(2)}) collective-permute-start(bf16[32,1280]{1,0:T(8,128)(2,1)S(1)} %collective-permute-done.3.refs_2_), channel_id=1, source_target_pairs={{0,1},{1,0},{2,3},{3,2},{4,5},{5,4},{6,7},{7,6},{8,9},{9,8},{10,11... | collective-permute-start | bytes 245768 | tf_op jit(solution)/shard_map/ppermute | solution.py:463
  24.6 3.3 %collective-permute-start.9 = (bf16[32,1280]{1,0:T(8,128)(2,1)S(1)}, bf16[32,1280]{1,0:T(8,128)(2,1)S(1)}, u32[]{:S(2)}, u32[]{:S(2)}) collective-permute-start(bf16[32,1280]{1,0:T(8,128)(2,1)S(1)} %collective-permute-done.4.refs_3_), channel_id=1, source_target_pairs={{0,1},{1,0},{2,3},{3,2},{4,5},{5,4},{6,7},{7,6},{8,9},{9,8},{10,11... | collective-permute-start | bytes 245768 | tf_op jit(solution)/shard_map/ppermute | solution.py:463
  24.9 4.2 %collective-permute-start.10 = (bf16[32,1280]{1,0:T(8,128)(2,1)S(1)}, bf16[32,1280]{1,0:T(8,128)(2,1)S(1)}, u32[]{:S(2)}, u32[]{:S(2)}) collective-permute-start(bf16[32,1280]{1,0:T(8,128)(2,1)S(1)} %collective-permute-done.5.refs_4_), channel_id=1, source_target_pairs={{0,1},{1,0},{2,3},{3,2},{4,5},{5,4},{6,7},{7,6},{8,9},{9,8},{10,11... | collective-permute-start | bytes 245768 | tf_op jit(solution)/shard_map/ppermute | solution.py:463
  25.1 4.5 %collective-permute-start.11 = (bf16[32,1280]{1,0:T(8,128)(2,1)S(1)}, bf16[32,1280]{1,0:T(8,128)(2,1)S(1)}, u32[]{:S(2)}, u32[]{:S(2)}) collective-permute-start(bf16[32,1280]{1,0:T(8,128)(2,1)S(1)} %collective-permute-done.6.refs_5_), channel_id=1, source_target_pairs={{0,1},{1,0},{2,3},{3,2},{4,5},{5,4},{6,7},{7,6},{8,9},{9,8},{10,11... | collective-permute-start | bytes 245768 | tf_op jit(solution)/shard_map/ppermute | solution.py:463
  25.4 9.8 %collective-permute-start.1 = (bf16[32,1280]{1,0:T(8,128)(2,1)S(1)}, bf16[32,1280]{1,0:T(8,128)(2,1)S(1)}, u32[]{:S(2)}, u32[]{:S(2)}) collective-permute-start(bf16[32,1280]{1,0:T(8,128)(2,1)S(1)} %get-tuple-element.19), channel_id=1, source_target_pairs={{0,20},{4,16},{8,28},{12,24},{16,4},{20,0},{24,12},{28,8},{1,21},{... | collective-permute-start | bytes 245768 | tf_op jit(solution)/shard_map/ppermute | solution.py:457
  28.0 7.2 %collective-permute-start.2 = (bf16[32,1280]{1,0:T(8,128)(2,1)S(1)}, bf16[32,1280]{1,0:T(8,128)(2,1)S(1)}, u32[]{:S(2)}, u32[]{:S(2)}) collective-permute-start(bf16[32,1280]{1,0:T(8,128)(2,1)S(1)} %get-tuple-element.20), channel_id=1, source_target_pairs={{0,4},{4,0},{8,12},{12,8},{16,20},{20,16},{24,28},{28,24},{1,5},{5... | collective-permute-start | bytes 245768 | tf_op jit(solution)/shard_map/ppermute | solution.py:457
  29.0 6.6 %collective-permute-start = (s32[2,1,40]{2,1,0:T(1,128)S(1)}, s32[2,1,40]{2,1,0:T(1,128)S(1)}, u32[]{:S(2)}, u32[]{:S(2)}) collective-permute-start(s32[2,1,40]{2,1,0:T(1,128)S(1)} %copy-done.1), channel_id=1, source_target_pairs={{0,2},{1,3},{2,0},{3,1},{4,6},{5,7},{6,4},{7,5},{8,10},{9,11},{10,... | collective-permute-start | bytes 968 | tf_op jit(solution)/shard_map/ppermute | solution.py:451
  29.6 7.7 %collective-permute-start.12 = (bf16[32,1280]{1,0:T(8,128)(2,1)S(1)}, bf16[32,1280]{1,0:T(8,128)(2,1)S(1)}, u32[]{:S(2)}, u32[]{:S(2)}) collective-permute-start(bf16[32,1280]{1,0:T(8,128)(2,1)S(1)} %get-tuple-element.28), channel_id=1, source_target_pairs={{0,24},{4,28},{8,16},{12,20},{16,8},{20,12},{24,0},{28,4},{1,25},{... | collective-permute-start | bytes 245768 | tf_op jit(solution)/shard_map/ppermute | solution.py:457
  35.1 2.2 %collective-permute-start.14 = (bf16[32,1280]{1,0:T(8,128)(2,1)S(1)}, bf16[32,1280]{1,0:T(8,128)(2,1)S(1)}, u32[]{:S(2)}, u32[]{:S(2)}) collective-permute-start(bf16[32,1280]{1,0:T(8,128)(2,1)S(1)} %collective-permute-done.1.refs_1_), channel_id=1, source_target_pairs={{0,1},{1,0},{2,3},{3,2},{4,5},{5,4},{6,7},{7,6},{8,9},{9,8},{10,11... | collective-permute-start | bytes 245768 | tf_op jit(solution)/shard_map/ppermute | solution.py:463
  35.1 2.2 %collective-permute-start.15 = (bf16[32,1280]{1,0:T(8,128)(2,1)S(1)}, bf16[32,1280]{1,0:T(8,128)(2,1)S(1)}, u32[]{:S(2)}, u32[]{:S(2)}) collective-permute-start(bf16[32,1280]{1,0:T(8,128)(2,1)S(1)} %collective-permute-done.2.refs_2_), channel_id=1, source_target_pairs={{0,1},{1,0},{2,3},{3,2},{4,5},{5,4},{6,7},{7,6},{8,9},{9,8},{10,11... | collective-permute-start | bytes 245768 | tf_op jit(solution)/shard_map/ppermute | solution.py:463
  37.3 1.3 %collective-permute-start.16 = (bf16[32,1280]{1,0:T(8,128)(2,1)S(1)}, bf16[32,1280]{1,0:T(8,128)(2,1)S(1)}, u32[]{:S(2)}, u32[]{:S(2)}) collective-permute-start(bf16[32,1280]{1,0:T(8,128)(2,1)S(1)} %collective-permute-done.12.refs_3_), channel_id=1, source_target_pairs={{0,1},{1,0},{2,3},{3,2},{4,5},{5,4},{6,7},{7,6},{8,9},{9,8},{10,11... | collective-permute-start | bytes 245768 | tf_op jit(solution)/shard_map/ppermute | solution.py:463
  39.9 4.3 %collective-permute-start.17 = (bf16[2,2,16,512]{3,2,1,0:T(8,128)(2,1)S(1)}, bf16[2,2,16,512]{3,2,1,0:T(8,128)(2,1)S(1)}, u32[]{:S(2)}, u32[]{:S(2)}) collective-permute-start(bf16[2,2,16,512]{3,2,1,0:T(8,128)(2,1)S(1)} %coefficients.6), channel_id=1, source_target_pairs={{0,2},{1,3},{2,0},{3,1},{4,6},{5,7},{6,4},{7,5},{8,10},{9,11},{10,... | collective-permute-start | bytes 196616 | tf_op jit(solution)/shard_map/ppermute | solution.py:480

commit v3 on v2

--- a/solution.py
+++ b/solution.py
@@ -429,10 +429,9 @@
 
 def arrivals(groups):
     order = shift_order(groups)
-    crossing = [s for s in order if s >= groups // 2]
-    middle = [s for s in order[:-1] if s == 1 or s in crossing[2:]]
-    early = [s for s in order[:-1] if s not in middle]
-    return [0] + early, middle, order[-1:]
+    crossing = [s for s in order[1:] if s >= groups // 2]
+    early = [s for s in order if s not in crossing and s != 1]
+    return [0] + early, [1] + crossing[:-1], crossing[-1:]
 
 
 def per_device_fast(wavefield, u_factors, v_factors, tile_ranks, tile_offsets):

time: 59 us -> 59.6 us (1.010)
  waiting for transfers between devices: 11.2 us -> 13.1 us
  blocking collectives: 11.8 us -> 10.1 us
    ppermute x7, waiting for transfers between devices: 7.94 us -> 10.9 us  [per_device_fast(): own[shift] = lax.ppermute(sent[shift], 'freq', swap)]
    all_to_all x1, blocking collectives: 11.8 us -> 10.1 us  [per_device_fast(): lax.all_to_all(bands, 'freq', split_axis=0, concat_axis=0, tiled=True)]
    ppermute x1, waiting for transfers between devices: 1.94 us -> 1.3 us  [per_device_fast(): far = lax.ppermute(leaving, 'rows', across)]
  transfers between devices with their start and end apart: 18 -> 18, of which waited for: 7 -> 7; matrix products, arithmetic and copies ran while one was open for 1% -> 1% of each run, Pallas kernels for 26% -> 25%
where the time goes in v3:
time: 59.6 us; the launch traced here: 59.5 us
  Pallas kernels  19.1 us (32%)
  starting transfers between devices  16.5 us (28%)
  waiting for transfers between devices  13.1 us (22%)
  blocking collectives  10.1 us (17%)
    ppermute x7, starting transfers between devices, per_device_fast(): own[shift] = lax.ppermute(sent[shift], 'freq', swap)  11.1 us
    ppermute x7, waiting for transfers between devices, per_device_fast(): own[shift] = lax.ppermute(sent[shift], 'freq', swap)  10.9 us
    all_to_all x1, blocking collectives, per_device_fast(): lax.all_to_all(bands, 'freq', split_axis=0, concat_axis=0, tiled=True)  10.1 us
    pallas_call x1, Pallas kernels, transform(): pl.pallas_call(transform_kernel, in_specs=[pl.BlockSpec(memory_space=pltp...  9.56 us
    pallas_call x4, Pallas kernels, coefficients(): pl.pallas_call(functools.partial(coefficient_kernel, tuple(shifts), sides...  5.79 us
    ppermute x1, starting transfers between devices, per_device_fast(): v_far = lax.ppermute(v_own, 'rows', across)  3.04 us
    pallas_call x2, Pallas kernels, bands_of(): pl.pallas_call(functools.partial(band_kernel, add, at_near), in_specs=[SM...  2.13 us
    pallas_call x1, Pallas kernels, series_of(): pl.pallas_call(functools.partial(series_kernel, scale), in_specs=[VMEM] *...  1.66 us
  transfers between devices with their start and end apart: 18, of which 7 were waited for; matrix products, arithmetic and copies ran while one was open for 1% of the time, Pallas kernels for 25%

profile of v3, /device:TPU:0, one launch (start us, length us, event | category | flops | bytes accessed | tf_op | source)
XLA Modules:
  0.0 59.5 jit_solution(8949725780842533413)
XLA Ops:
  0.0 3.0 %collective-permute-start.12 = (bf16[2,2,512,256]{3,2,1,0:T(8,128)(2,1)}, bf16[2,2,512,256]{3,2,1,0:T(8,128)(2,1)S(1)}, u32[]{:S(2)}, u32[]{:S(2)}) collective-permute-start(bf16[2,2,512,256]{3,2,1,0:T(8,128)(2,1)} %bitcast.8), channel_id=1, source_target_pairs={{0,2},{1,3},{2,0},{3,1},{4,6},{5,7},{6,4},{7,5},{8,10},{9,11},{10,... | collective-permute-start | bytes 3145736 | tf_op jit(solution)/shard_map/ppermute | solution.py:449
  3.1 0.3 fusion.7
  3.4 0.1 copy.6
  3.6 9.6 %transform.1 = (bf16[32,1280]{1,0:T(8,128)(2,1)S(1)}, bf16[32,1280]{1,0:T(8,128)(2,1)S(1)}, bf16[32,1280]{1,0:T(8,128)(2,1)S(1)}, bf16[32,1280]{1,0:T(8,128)(2,1...) custom-call(bf16[10240,1024]{1,0:T(8,128)(2,1)} %bitcast.11, ...), custom_call_target="tpu_custom_call" | custom-call | flops 5368709120 | bytes 20971520 | tf_op jit(solution)/shard_map/transform/pallas_call | solution.py:185
  13.1 2.7 %collective-permute-start.4 = (bf16[32,1280]{1,0:T(8,128)(2,1)S(1)}, bf16[32,1280]{1,0:T(8,128)(2,1)S(1)}, u32[]{:S(2)}, u32[]{:S(2)}) collective-permute-start(bf16[32,1280]{1,0:T(8,128)(2,1)S(1)} %get-tuple-element.24), channel_id=1, source_target_pairs={{0,16},{4,20},{8,24},{12,28},{16,0},{20,4},{24,8},{28,12},{1,17},{... | collective-permute-start | bytes 245768 | tf_op jit(solution)/shard_map/ppermute | solution.py:456
  15.8 1.6 %collective-permute-start.5 = (bf16[32,1280]{1,0:T(8,128)(2,1)S(1)}, bf16[32,1280]{1,0:T(8,128)(2,1)S(1)}, u32[]{:S(2)}, u32[]{:S(2)}) collective-permute-start(bf16[32,1280]{1,0:T(8,128)(2,1)S(1)} %get-tuple-element.25), channel_id=1, source_target_pairs={{0,8},{4,12},{8,0},{12,4},{16,24},{20,28},{24,16},{28,20},{1,9},{5... | collective-permute-start | bytes 245768 | tf_op jit(solution)/shard_map/ppermute | solution.py:456
  17.4 1.4 %collective-permute-start.6 = (bf16[32,1280]{1,0:T(8,128)(2,1)S(1)}, bf16[32,1280]{1,0:T(8,128)(2,1)S(1)}, u32[]{:S(2)}, u32[]{:S(2)}) collective-permute-start(bf16[32,1280]{1,0:T(8,128)(2,1)S(1)} %get-tuple-element.26), channel_id=1, source_target_pairs={{0,12},{4,8},{8,4},{12,0},{16,28},{20,24},{24,20},{28,16},{1,13},{... | collective-permute-start | bytes 245768 | tf_op jit(solution)/shard_map/ppermute | solution.py:456
  18.8 0.0 collective-permute-start.7
  18.8 0.5 collective-permute-done.4.refs_2_
  19.3 1.3 %collective-permute-done.5.refs_3_ = bf16[32,1280]{1,0:T(8,128)(2,1)S(1)} collective-permute-done((bf16[32,1280]{1,0:T(8,128)(2,1)S(1)}, bf16[32,1280]{1,0:T(8,128)(2,1)S(1)}, u32[]{:S(2)}, u32[]{:S(2)}) %collective-permute-start.5) | collective-permute-done | bytes 81952 | tf_op jit(solution)/shard_map/ppermute | solution.py:456
  20.7 2.3 %collective-permute-done.6.refs_4_ = bf16[32,1280]{1,0:T(8,128)(2,1)S(1)} collective-permute-done((bf16[32,1280]{1,0:T(8,128)(2,1)S(1)}, bf16[32,1280]{1,0:T(8,128)(2,1)S(1)}, u32[]{:S(2)}, u32[]{:S(2)}) %collective-permute-start.6) | collective-permute-done | bytes 81952 | tf_op jit(solution)/shard_map/ppermute | solution.py:456
  23.0 1.2 %collective-permute-start.1 = (bf16[32,1280]{1,0:T(8,128)(2,1)S(1)}, bf16[32,1280]{1,0:T(8,128)(2,1)S(1)}, u32[]{:S(2)}, u32[]{:S(2)}) collective-permute-start(bf16[32,1280]{1,0:T(8,128)(2,1)S(1)} %get-tuple-element.20), channel_id=1, source_target_pairs={{0,4},{4,0},{8,12},{12,8},{16,20},{20,16},{24,28},{28,24},{1,5},{5... | collective-permute-start | bytes 245768 | tf_op jit(solution)/shard_map/ppermute | solution.py:456
  24.2 2.5 %collective-permute-start.2 = (bf16[32,1280]{1,0:T(8,128)(2,1)S(1)}, bf16[32,1280]{1,0:T(8,128)(2,1)S(1)}, u32[]{:S(2)}, u32[]{:S(2)}) collective-permute-start(bf16[32,1280]{1,0:T(8,128)(2,1)S(1)} %get-tuple-element.21), channel_id=1, source_target_pairs={{0,28},{4,24},{8,20},{12,16},{16,12},{20,8},{24,4},{28,0},{1,29},{... | collective-permute-start | bytes 245768 | tf_op jit(solution)/shard_map/ppermute | solution.py:456
  26.7 0.7 %collective-permute-start.3 = (bf16[32,1280]{1,0:T(8,128)(2,1)S(1)}, bf16[32,1280]{1,0:T(8,128)(2,1)S(1)}, u32[]{:S(2)}, u32[]{:S(2)}) collective-permute-start(bf16[32,1280]{1,0:T(8,128)(2,1)S(1)} %get-tuple-element.22), channel_id=1, source_target_pairs={{0,20},{4,16},{8,28},{12,24},{16,4},{20,0},{24,12},{28,8},{1,21},{... | collective-permute-start | bytes 245768 | tf_op jit(solution)/shard_map/ppermute | solution.py:456
  27.5 1.0 %collective-permute-start.11 = (bf16[32,1280]{1,0:T(8,128)(2,1)S(1)}, bf16[32,1280]{1,0:T(8,128)(2,1)S(1)}, u32[]{:S(2)}, u32[]{:S(2)}) collective-permute-start(bf16[32,1280]{1,0:T(8,128)(2,1)S(1)} %get-tuple-element.30), channel_id=1, source_target_pairs={{0,24},{4,28},{8,16},{12,20},{16,8},{20,12},{24,0},{28,4},{1,25},{... | collective-permute-start | bytes 245768 | tf_op jit(solution)/shard_map/ppermute | solution.py:456
  28.5 1.4 %coefficients.4.refs_10_ = bf16[2,2,16,512]{3,2,1,0:T(8,128)(2,1)S(1)} custom-call(s32[2,1,40]{2,1,0:T(1,128)S(1)} %copy-done.1, bf16[32,1280]{1,0:T(8,128)(2,1)S(1)} %get-tuple-element.23.refs_1_, bf16[32,1280]{1,0:T(8,128)(2,1)S(1)} %collective-permute-done.4.refs_2_, bf16[32,1280]{1,0:T(8,128)(2,1)S(1)} %collective-permute-done.5.refs_3_, ...), custom_call_target="tpu_custom_call" | custom-call | flops 671088640 | bytes 1048576 | tf_op jit(solution)/shard_map/coefficients/pallas_call | solution.py:275
  30.0 0.6 %collective-permute-start = (s32[2,1,40]{2,1,0:T(1,128)S(1)}, s32[2,1,40]{2,1,0:T(1,128)S(1)}, u32[]{:S(2)}, u32[]{:S(2)}) collective-permute-start(s32[2,1,40]{2,1,0:T(1,128)S(1)} %copy-done.1), channel_id=1, source_target_pairs={{0,2},{1,3},{2,0},{3,1},{4,6},{5,7},{6,4},{7,5},{8,10},{9,11},{10,... | collective-permute-start | bytes 968 | tf_op jit(solution)/shard_map/ppermute | solution.py:450
  30.6 1.8 %collective-permute-done.2.refs_2_ = bf16[32,1280]{1,0:T(8,128)(2,1)S(1)} collective-permute-done((bf16[32,1280]{1,0:T(8,128)(2,1)S(1)}, bf16[32,1280]{1,0:T(8,128)(2,1)S(1)}, u32[]{:S(2)}, u32[]{:S(2)}) %collective-permute-start.2) | collective-permute-done | bytes 81952 | tf_op jit(solution)/shard_map/ppermute | solution.py:456
  32.3 4.9 %collective-permute-done.3.refs_3_ = bf16[32,1280]{1,0:T(8,128)(2,1)S(1)} collective-permute-done((bf16[32,1280]{1,0:T(8,128)(2,1)S(1)}, bf16[32,1280]{1,0:T(8,128)(2,1)S(1)}, u32[]{:S(2)}, u32[]{:S(2)}) %collective-permute-start.3) | collective-permute-done | bytes 81952 | tf_op jit(solution)/shard_map/ppermute | solution.py:456
  37.3 0.5 collective-permute-start.14
  37.8 0.0 collective-permute-start.15
  37.8 1.5 %coefficients.5.refs_10_ = bf16[2,2,16,512]{3,2,1,0:T(8,128)(2,1)S(1)} custom-call(s32[2,1,40]{2,1,0:T(1,128)S(1)} %collective-permute-done.refs_0_, bf16[32,1280]{1,0:T(8,128)(2,1)S(1)} %get-tuple-element.23.refs_1_, bf16[32,1280]{1,0:T(8,128)(2,1)S(1)} %collective-permute-done.4.refs_2_, bf16[32,1280]{1,0:T(8,128)(2,1)S(1)} %collective-permute-done.5.refs_3_, ...), custom_call_target="tpu_custom_call" | custom-call | flops 671088640 | bytes 1048576 | tf_op jit(solution)/shard_map/coefficients/pallas_call | solution.py:275
  39.3 0.6 collective-permute-start.16
  39.8 0.9 %collective-permute-done.16.refs_8_ = bf16[32,1280]{1,0:T(8,128)(2,1)S(1)} collective-permute-done((bf16[32,1280]{1,0:T(8,128)(2,1)S(1)}, bf16[32,1280]{1,0:T(8,128)(2,1)S(1)}, u32[]{:S(2)}, u32[]{:S(2)}) %collective-permute-start.16) | collective-permute-done | bytes 81952 | tf_op jit(solution)/shard_map/ppermute | solution.py:462
  40.8 1.4 %coefficients.6 = bf16[2,2,16,512]{3,2,1,0:T(8,128)(2,1)S(1)} custom-call(s32[2,1,40]{2,1,0:T(1,128)S(1)} %collective-permute-done.refs_0_, bf16[32,1280]{1,0:T(8,128)(2,1)S(1)} %collective-permute-done.1.refs_1_, bf16[32,1280]{1,0:T(8,128)(2,1)S(1)} %collective-permute-done.2.refs_2_, bf16[32,1280]{1,0:T(8,128)(2,1)S(1)} %collective-permute-done.3.refs_3_, ...), custom_call_target="tpu_custom_call" | custom-call | flops 671088640 | bytes 1048576 | tf_op jit(solution)/shard_map/coefficients/pallas_call | solution.py:275
  42.2 0.6 %collective-permute-start.17 = (bf16[2,2,16,512]{3,2,1,0:T(8,128)(2,1)S(1)}, bf16[2,2,16,512]{3,2,1,0:T(8,128)(2,1)S(1)}, u32[]{:S(2)}, u32[]{:S(2)}) collective-permute-start(bf16[2,2,16,512]{3,2,1,0:T(8,128)(2,1)S(1)} %coefficients.6), channel_id=1, source_target_pairs={{0,2},{1,3},{2,0},{3,1},{4,6},{5,7},{6,4},{7,5},{8,10},{9,11},{10,... | collective-permute-start | bytes 196616 | tf_op jit(solution)/shard_map/ppermute | solution.py:479
  42.8 1.4 %coefficients.7.coeffs_ref = bf16[2,2,16,512]{3,2,1,0:T(8,128)(2,1)S(1)} custom-call(s32[2,1,40]{2,1,0:T(1,128)S(1)} %copy-done.1, bf16[32,1280]{1,0:T(8,128)(2,1)S(1)} %collective-permute-done.1.refs_1_, bf16[32,1280]{1,0:T(8,128)(2,1)S(1)} %collective-permute-done.2.refs_2_, bf16[32,1280]{1,0:T(8,128)(2,1)S(1)} %collective-permute-done.3.refs_3_, ...), custom_call_target="tpu_custom_call" | custom-call | flops 671088640 | bytes 1048576 | tf_op jit(solution)/shard_map/coefficients/pallas_call | solution.py:275
  44.3 1.0 %bands.2.refs_0_ = f32[256,128]{1,0:T(8,128)S(1)} custom-call(s32[2,1,40]{2,1,0:T(1,128)S(1)} %copy-done.1, s32[2,1,40]{2,1,0:T(1,128)S(1)} %copy-done.2, bf16[2,2,16,512]{3,2,1,0:T(8,128)(2,1)S(1)} %coefficients.7.coeffs_ref, bf16[2,2,256,512]{3,2,1,0:T(8,128)(2,1)S(1)} %bitcast.5), custom_call_target="tpu_custom_call" | custom-call | flops 134217728 | bytes 1048576 | tf_op jit(solution)/shard_map/bands/pallas_call | solution.py:347
  45.3 1.3 %collective-permute-done.17.coeffs_ref = bf16[2,2,16,512]{3,2,1,0:T(8,128)(2,1)S(1)} collective-permute-done((bf16[2,2,16,512]{3,2,1,0:T(8,128)(2,1)S(1)}, bf16[2,2,16,512]{3,2,1,0:T(8,128)(2,1)S(1)}, u32[]{:S(2)}, u32[]{:S(2)}) %collective-permute-start.17) | collective-permute-done | bytes 65568 | tf_op jit(solution)/shard_map/ppermute | solution.py:479
  46.6 1.1 %bands.3 = bf16[8,32,128]{2,1,0:T(8,128)(2,1)S(1)} custom-call(s32[2,1,40]{2,1,0:T(1,128)S(1)} %copy-done.1, s32[2,1,40]{2,1,0:T(1,128)S(1)} %copy-done.2, bf16[2,2,16,512]{3,2,1,0:T(8,128)(2,1)S(1)} %collective-permute-done.17.coeffs_ref, bf16[2,2,256,512]{3,2,1,0:T(8,128)(2,1)S(1)} %bitcast.6, f32[256,128]{1,0:T(8,128)S(1)} %bands.2.refs_0_), custom_call_target="tpu_custom_call" | custom-call | flops 134217728 | bytes 1048576 | tf_op jit(solution)/shard_map/bands/pallas_call | solution.py:347
  47.8 10.1 %all_to_all.5.bands_ref = bf16[8,32,128]{2,1,0:T(8,128)(2,1)S(1)} all-to-all(bf16[8,32,128]{2,1,0:T(8,128)(2,1)S(1)} %bands.3), channel_id=1, replica_groups=mesh['freq'=8,'rows'=4] {'freq'}, dimensions={0} | all-to-all | bytes 131072 | tf_op jit(solution)/shard_map/all_to_all | solution.py:483
  57.8 1.7 %series.1 = bf16[1024,1024]{1,0:T(8,128)(2,1)} custom-call(bf16[8,32,128]{2,1,0:T(8,128)(2,1)S(1)} %all_to_all.5.bands_ref, bf16[32,1024]{1,0:T(8,128)(2,1)S(1)} %convert_element_type.29.table_ref), custom_call_target="tpu_custom_call" | custom-call | flops 67108864 | bytes 2097152 | tf_op jit(solution)/shard_map/series/pallas_call | solution.py:386
  (27 shorter events, 0.1 us)
Async XLA Ops:
  0.0 28.5 %copy-start.3 = (bf16[2,2,1,512,256]{4,3,2,1,0:T(8,128)(2,1)S(1)}, bf16[2,2,1,512,256]{4,3,2,1,0:T(8,128)(2,1)}, u32[]{:S(2)}) copy-start(bf16[2,2,1,512,256]{4,3,2,1,0:T(8,128)(2,1)} %param.7) | copy-start | bytes 3145732
  0.0 28.5 %copy-start.1 = (s32[2,1,40]{2,1,0:T(1,128)S(1)}, s32[2,1,40]{2,1,0:T(1,128)}, u32[]{:S(2)}) copy-start(s32[2,1,40]{2,1,0:T(1,128)} %offsets_ref.3) | copy-start | bytes 964
  0.0 44.3 %copy-start.2 = (s32[2,1,40]{2,1,0:T(1,128)S(1)}, s32[2,1,40]{2,1,0:T(1,128)}, u32[]{:S(2)}) copy-start(s32[2,1,40]{2,1,0:T(1,128)} %ranks_ref.3) | copy-start | bytes 964
  0.0 44.3 %copy-start = (bf16[2,2,1,256,512]{4,3,2,1,0:T(8,128)(2,1)S(1)}, bf16[2,2,1,256,512]{4,3,2,1,0:T(8,128)(2,1)}, u32[]{:S(2)}) copy-start(bf16[2,2,1,256,512]{4,3,2,1,0:T(8,128)(2,1)} %param.6) | copy-start | bytes 3145732
  0.0 37.8 %collective-permute-start.12 = (bf16[2,2,512,256]{3,2,1,0:T(8,128)(2,1)}, bf16[2,2,512,256]{3,2,1,0:T(8,128)(2,1)S(1)}, u32[]{:S(2)}, u32[]{:S(2)}) collective-permute-start(bf16[2,2,512,256]{3,2,1,0:T(8,128)(2,1)} %bitcast.8), channel_id=1, source_target_pairs={{0,2},{1,3},{2,0},{3,1},{4,6},{5,7},{6,4},{7,5},{8,10},{9,11},{10,... | collective-permute-start | bytes 3145736 | tf_op jit(solution)/shard_map/ppermute | solution.py:449
  13.1 6.2 %collective-permute-start.4 = (bf16[32,1280]{1,0:T(8,128)(2,1)S(1)}, bf16[32,1280]{1,0:T(8,128)(2,1)S(1)}, u32[]{:S(2)}, u32[]{:S(2)}) collective-permute-start(bf16[32,1280]{1,0:T(8,128)(2,1)S(1)} %get-tuple-element.24), channel_id=1, source_target_pairs={{0,16},{4,20},{8,24},{12,28},{16,0},{20,4},{24,8},{28,12},{1,17},{... | collective-permute-start | bytes 245768 | tf_op jit(solution)/shard_map/ppermute | solution.py:456
  15.8 4.9 %collective-permute-start.5 = (bf16[32,1280]{1,0:T(8,128)(2,1)S(1)}, bf16[32,1280]{1,0:T(8,128)(2,1)S(1)}, u32[]{:S(2)}, u32[]{:S(2)}) collective-permute-start(bf16[32,1280]{1,0:T(8,128)(2,1)S(1)} %get-tuple-element.25), channel_id=1, source_target_pairs={{0,8},{4,12},{8,0},{12,4},{16,24},{20,28},{24,16},{28,20},{1,9},{5... | collective-permute-start | bytes 245768 | tf_op jit(solution)/shard_map/ppermute | solution.py:456
  17.4 5.6 %collective-permute-start.6 = (bf16[32,1280]{1,0:T(8,128)(2,1)S(1)}, bf16[32,1280]{1,0:T(8,128)(2,1)S(1)}, u32[]{:S(2)}, u32[]{:S(2)}) collective-permute-start(bf16[32,1280]{1,0:T(8,128)(2,1)S(1)} %get-tuple-element.26), channel_id=1, source_target_pairs={{0,12},{4,8},{8,4},{12,0},{16,28},{20,24},{24,20},{28,16},{1,13},{... | collective-permute-start | bytes 245768 | tf_op jit(solution)/shard_map/ppermute | solution.py:456
  18.8 4.2 %collective-permute-start.7 = (bf16[32,1280]{1,0:T(8,128)(2,1)S(1)}, bf16[32,1280]{1,0:T(8,128)(2,1)S(1)}, u32[]{:S(2)}, u32[]{:S(2)}) collective-permute-start(bf16[32,1280]{1,0:T(8,128)(2,1)S(1)} %get-tuple-element.23.refs_1_), channel_id=1, source_target_pairs={{0,1},{1,0},{2,3},{3,2},{4,5},{5,4},{6,7},{7,6},{8,9},{9,8},{10,11... | collective-permute-start | bytes 245768 | tf_op jit(solution)/shard_map/ppermute | solution.py:462
  19.3 4.9 %collective-permute-start.8 = (bf16[32,1280]{1,0:T(8,128)(2,1)S(1)}, bf16[32,1280]{1,0:T(8,128)(2,1)S(1)}, u32[]{:S(2)}, u32[]{:S(2)}) collective-permute-start(bf16[32,1280]{1,0:T(8,128)(2,1)S(1)} %collective-permute-done.4.refs_2_), channel_id=1, source_target_pairs={{0,1},{1,0},{2,3},{3,2},{4,5},{5,4},{6,7},{7,6},{8,9},{9,8},{10,11... | collective-permute-start | bytes 245768 | tf_op jit(solution)/shard_map/ppermute | solution.py:462
  20.7 6.1 %collective-permute-start.9 = (bf16[32,1280]{1,0:T(8,128)(2,1)S(1)}, bf16[32,1280]{1,0:T(8,128)(2,1)S(1)}, u32[]{:S(2)}, u32[]{:S(2)}) collective-permute-start(bf16[32,1280]{1,0:T(8,128)(2,1)S(1)} %collective-permute-done.5.refs_3_), channel_id=1, source_target_pairs={{0,1},{1,0},{2,3},{3,2},{4,5},{5,4},{6,7},{7,6},{8,9},{9,8},{10,11... | collective-permute-start | bytes 245768 | tf_op jit(solution)/shard_map/ppermute | solution.py:462
  23.0 4.5 %collective-permute-start.10 = (bf16[32,1280]{1,0:T(8,128)(2,1)S(1)}, bf16[32,1280]{1,0:T(8,128)(2,1)S(1)}, u32[]{:S(2)}, u32[]{:S(2)}) collective-permute-start(bf16[32,1280]{1,0:T(8,128)(2,1)S(1)} %collective-permute-done.6.refs_4_), channel_id=1, source_target_pairs={{0,1},{1,0},{2,3},{3,2},{4,5},{5,4},{6,7},{7,6},{8,9},{9,8},{10,11... | collective-permute-start | bytes 245768 | tf_op jit(solution)/shard_map/ppermute | solution.py:462
  23.0 6.9 %collective-permute-start.1 = (bf16[32,1280]{1,0:T(8,128)(2,1)S(1)}, bf16[32,1280]{1,0:T(8,128)(2,1)S(1)}, u32[]{:S(2)}, u32[]{:S(2)}) collective-permute-start(bf16[32,1280]{1,0:T(8,128)(2,1)S(1)} %get-tuple-element.20), channel_id=1, source_target_pairs={{0,4},{4,0},{8,12},{12,8},{16,20},{20,16},{24,28},{28,24},{1,5},{5... | collective-permute-start | bytes 245768 | tf_op jit(solution)/shard_map/ppermute | solution.py:456
  24.2 8.1 %collective-permute-start.2 = (bf16[32,1280]{1,0:T(8,128)(2,1)S(1)}, bf16[32,1280]{1,0:T(8,128)(2,1)S(1)}, u32[]{:S(2)}, u32[]{:S(2)}) collective-permute-start(bf16[32,1280]{1,0:T(8,128)(2,1)S(1)} %get-tuple-element.21), channel_id=1, source_target_pairs={{0,28},{4,24},{8,20},{12,16},{16,12},{20,8},{24,4},{28,0},{1,29},{... | collective-permute-start | bytes 245768 | tf_op jit(solution)/shard_map/ppermute | solution.py:456
  26.7 10.5 %collective-permute-start.3 = (bf16[32,1280]{1,0:T(8,128)(2,1)S(1)}, bf16[32,1280]{1,0:T(8,128)(2,1)S(1)}, u32[]{:S(2)}, u32[]{:S(2)}) collective-permute-start(bf16[32,1280]{1,0:T(8,128)(2,1)S(1)} %get-tuple-element.22), channel_id=1, source_target_pairs={{0,20},{4,16},{8,28},{12,24},{16,4},{20,0},{24,12},{28,8},{1,21},{... | collective-permute-start | bytes 245768 | tf_op jit(solution)/shard_map/ppermute | solution.py:456
  27.5 11.8 %collective-permute-start.11 = (bf16[32,1280]{1,0:T(8,128)(2,1)S(1)}, bf16[32,1280]{1,0:T(8,128)(2,1)S(1)}, u32[]{:S(2)}, u32[]{:S(2)}) collective-permute-start(bf16[32,1280]{1,0:T(8,128)(2,1)S(1)} %get-tuple-element.30), channel_id=1, source_target_pairs={{0,24},{4,28},{8,16},{12,20},{16,8},{20,12},{24,0},{28,4},{1,25},{... | collective-permute-start | bytes 245768 | tf_op jit(solution)/shard_map/ppermute | solution.py:456
  30.0 7.8 %collective-permute-start = (s32[2,1,40]{2,1,0:T(1,128)S(1)}, s32[2,1,40]{2,1,0:T(1,128)S(1)}, u32[]{:S(2)}, u32[]{:S(2)}) collective-permute-start(s32[2,1,40]{2,1,0:T(1,128)S(1)} %copy-done.1), channel_id=1, source_target_pairs={{0,2},{1,3},{2,0},{3,1},{4,6},{5,7},{6,4},{7,5},{8,10},{9,11},{10,... | collective-permute-start | bytes 968 | tf_op jit(solution)/shard_map/ppermute | solution.py:450
  37.3 2.6 %collective-permute-start.13 = (bf16[32,1280]{1,0:T(8,128)(2,1)S(1)}, bf16[32,1280]{1,0:T(8,128)(2,1)S(1)}, u32[]{:S(2)}, u32[]{:S(2)}) collective-permute-start(bf16[32,1280]{1,0:T(8,128)(2,1)S(1)} %collective-permute-done.1.refs_1_), channel_id=1, source_target_pairs={{0,1},{1,0},{2,3},{3,2},{4,5},{5,4},{6,7},{7,6},{8,9},{9,8},{10,11... | collective-permute-start | bytes 245768 | tf_op jit(solution)/shard_map/ppermute | solution.py:462
  37.3 2.6 %collective-permute-start.14 = (bf16[32,1280]{1,0:T(8,128)(2,1)S(1)}, bf16[32,1280]{1,0:T(8,128)(2,1)S(1)}, u32[]{:S(2)}, u32[]{:S(2)}) collective-permute-start(bf16[32,1280]{1,0:T(8,128)(2,1)S(1)} %collective-permute-done.2.refs_2_), channel_id=1, source_target_pairs={{0,1},{1,0},{2,3},{3,2},{4,5},{5,4},{6,7},{7,6},{8,9},{9,8},{10,11... | collective-permute-start | bytes 245768 | tf_op jit(solution)/shard_map/ppermute | solution.py:462
  37.8 2.1 %collective-permute-start.15 = (bf16[32,1280]{1,0:T(8,128)(2,1)S(1)}, bf16[32,1280]{1,0:T(8,128)(2,1)S(1)}, u32[]{:S(2)}, u32[]{:S(2)}) collective-permute-start(bf16[32,1280]{1,0:T(8,128)(2,1)S(1)} %collective-permute-done.3.refs_3_), channel_id=1, source_target_pairs={{0,1},{1,0},{2,3},{3,2},{4,5},{5,4},{6,7},{7,6},{8,9},{9,8},{10,11... | collective-permute-start | bytes 245768 | tf_op jit(solution)/shard_map/ppermute | solution.py:462
  39.3 1.5 %collective-permute-start.16 = (bf16[32,1280]{1,0:T(8,128)(2,1)S(1)}, bf16[32,1280]{1,0:T(8,128)(2,1)S(1)}, u32[]{:S(2)}, u32[]{:S(2)}) collective-permute-start(bf16[32,1280]{1,0:T(8,128)(2,1)S(1)} %collective-permute-done.11.refs_4_), channel_id=1, source_target_pairs={{0,1},{1,0},{2,3},{3,2},{4,5},{5,4},{6,7},{7,6},{8,9},{9,8},{10,11... | collective-permute-start | bytes 245768 | tf_op jit(solution)/shard_map/ppermute | solution.py:462
  42.2 4.4 %collective-permute-start.17 = (bf16[2,2,16,512]{3,2,1,0:T(8,128)(2,1)S(1)}, bf16[2,2,16,512]{3,2,1,0:T(8,128)(2,1)S(1)}, u32[]{:S(2)}, u32[]{:S(2)}) collective-permute-start(bf16[2,2,16,512]{3,2,1,0:T(8,128)(2,1)S(1)} %coefficients.6), channel_id=1, source_target_pairs={{0,2},{1,3},{2,0},{3,1},{4,6},{5,7},{6,4},{7,5},{8,10},{9,11},{10,... | collective-permute-start | bytes 196616 | tf_op jit(solution)/shard_map/ppermute | solution.py:479
